TPU v7x, 256 devices: a whole 4x4x8 slice. The times are simulated.
256 devices in a mesh: replica: 8 (over y, x_lo), fsdp: 32 (over z, x_hi, core).
Axes of the slice: x: 4 (x_hi: 2, x_lo: 2; x = x_hi * 2 + x_lo), y: 4, z: 8, core: 2. Of those that a mesh axis runs over, the one named last changes fastest.
Arguments:
- codes: int32 [8, 8192, 4096], P('replica', None, 'fsdp'), may hold values from -127 to 127
- scales: float32 [8, 32, 8192], P('replica', 'fsdp'), may hold values from 0.002 to 0.03
- master: float32 [8192, 4096], P(('replica', 'fsdp')), may hold values from -6 to 6
- momentum: float32 [8192, 4096], P(('replica', 'fsdp')), may hold values from -6 to 6
Outputs:
- new_master: float32 [8192, 4096], P(('replica', 'fsdp'))
- new_momentum: float32 [8192, 4096], P(('replica', 'fsdp'))
- weights: bfloat16 [8192, 4096], P(None, 'fsdp')
All inputs are finite; a program needn't handle non-finite values.
Results may differ from a plain program's by a relative error of at most 0.0075.
Values may be sent and summed in bfloat16 or wider, within the bound.
No kernel may reach another device: no remote copies, remote signals or barrier semaphores. Data moves between devices by JAX's collectives and lax.ppermute only.
A program may use at most 64 MiB of HBM per device.

v0:
```python
import jax
import jax.numpy as jnp
from jax import lax
from jax.sharding import PartitionSpec as P

outer_rate = 0.7
momentum_factor = 0.9


def in_blocks(x, dim, size):
    lengths = x.shape
    parts = x.reshape(*lengths[:dim], size, lengths[dim] // size, *lengths[dim + 1 :])
    return jnp.moveaxis(parts, dim, 0)


def edges_of(length, count):
    unit = 8 if length >= 8 * count else 1
    return [length // unit * k // count * unit for k in range(1, count)]


def laid_out(parts, dim):
    parts = jnp.moveaxis(parts, 0, dim)
    lengths = parts.shape
    return parts.reshape(*lengths[:dim], lengths[dim] * lengths[dim + 1], *lengths[dim + 2 :])


def several_exchanges(x, axis, pieces, split_dim, concat_dim):
    parts = in_blocks(x, split_dim, lax.axis_size(axis))
    cut = max(range(1, max(2, parts.ndim - 1)), key=lambda d: parts.shape[d])
    finished = []
    for slab in jnp.split(parts, edges_of(parts.shape[cut], pieces), axis=cut):
        if slab.size:
            finished.append(lax.all_to_all(slab, axis, split_axis=0, concat_axis=0, tiled=True))
    return laid_out(jnp.concatenate(finished, axis=cut), concat_dim)


def copy_for_each(x, axis):
    size = lax.axis_size(axis)
    return lax.all_to_all(jnp.broadcast_to(x[None], (size, *x.shape)), axis, 0, 0, tiled=True)


def collect(x, axis, dim):
    parts = copy_for_each(x, axis)
    return laid_out(parts, dim)


def outer_update(summed, master, momentum, replica_count):
    mean_delta = summed / replica_count
    new_momentum = momentum_factor * momentum + mean_delta
    new_master = master - outer_rate * (mean_delta + momentum_factor * new_momentum)
    return (new_master, new_momentum)


def local(codes, scales, master, momentum):
    replica_count = lax.axis_size("replica")
    width = codes.shape[2]
    block_count = scales.shape[1]
    code_rows = codes.astype(jnp.bfloat16)
    scale_rows = jnp.transpose(scales, (0, 2, 1))
    got_codes, got_scales = (
        several_exchanges(code_rows, "replica", 2, 1, 0),
        several_exchanges(scale_rows.astype(jnp.bfloat16), "replica", 2, 1, 0).astype(
            scale_rows.dtype
        ),
    )
    group_rows = got_codes.shape[1]
    scaled = got_codes.astype(jnp.float32).reshape(
        replica_count, group_rows, block_count, width // block_count
    )
    scaled = scaled * got_scales[:, :, :, None]
    partial_sum = jnp.sum(scaled, axis=0).reshape(group_rows, width)
    summed = lax.all_to_all(
        partial_sum.astype(jnp.bfloat16), "fsdp", split_axis=0, concat_axis=1, tiled=True
    ).astype(partial_sum.dtype)
    new_master, new_momentum = outer_update(summed, master, momentum, replica_count)
    rounded = new_master.astype(jnp.bfloat16)
    columns = lax.all_to_all(rounded, "fsdp", split_axis=1, concat_axis=0, tiled=True)
    weights = collect(columns, "replica", 0)
    return (new_master, new_momentum, weights)


def solution(mesh):
    return jax.shard_map(
        local,
        mesh=mesh,
        in_specs=(
            P("replica", None, "fsdp"),
            P("replica", "fsdp", None),
            P(("replica", "fsdp"), None),
            P(("replica", "fsdp"), None),
        ),
        out_specs=(P(("replica", "fsdp"), None), P(("replica", "fsdp"), None), P(None, "fsdp")),
        check_vma=False,
    )
```

profile of v0, /device:TPU:1, one launch (start us, length us, event | category | flops | bytes accessed | tf_op | source)
XLA Modules:
  0.0 132.5 jit_solution(683285282375513844)
XLA Ops:
  0.6 0.8 convert_element_type.61
  1.5 0.5 broadcast.22
  2.0 0.7 reduce.1
  2.7 0.6 reshape.73
  3.3 5.9 %all-to-all-start.3 = ((bf16[8,2,256]{2,1,0:T(2,128)(2,1)}), bf16[8,2,256]{2,1,0:T(2,128)(2,1)S(1)}, u32[]{:S(2)}, u32[]{:S(2)}) async-start(bf16[8,2,256]{2,1,0:T(2,128)(2,1)} %reshape.73), calls=%async_computation.3 | async-start | bytes 16384 | tf_op jit(solution)/shard_map/all_to_all | solution.py:33
  9.2 0.7 reduce.2
  9.9 0.6 reshape.75
  10.5 2.4 %convert_element_type.58 = bf16[1,8192,128]{2,1,0:T(8,128)(2,1)S(1)} convert(s32[1,8192,128]{2,1,0:T(8,128)} %param.4) | non-fusion elementwise | flops 1048576 | bytes 6291456 | tf_op jit(solution)/shard_map/convert_element_type | solution.py:58
  12.9 1.3 %all-to-all-done.3 = bf16[8,2,256]{2,1,0:T(2,128)(2,1)S(1)} async-done(((bf16[8,2,256]{2,1,0:T(2,128)(2,1)}), bf16[8,2,256]{2,1,0:T(2,128)(2,1)S(1)}, u32[]{:S(2)}, u32[]{:S(2)}) %all-to-all-start.3) | async-done | bytes 8224 | tf_op jit(solution)/shard_map/all_to_all | solution.py:33
  14.3 3.8 %all-to-all-start.2 = ((bf16[8,2,256]{2,1,0:T(2,128)(2,1)}), bf16[8,2,256]{2,1,0:T(2,128)(2,1)S(1)}, u32[]{:S(2)}, u32[]{:S(2)}) async-start(bf16[8,2,256]{2,1,0:T(2,128)(2,1)} %reshape.75), calls=%async_computation.2 | async-start | bytes 16384 | tf_op jit(solution)/shard_map/all_to_all | solution.py:33
  18.1 1.1 fusion.4
  19.2 3.9 %all-to-all-done.2 = bf16[8,2,256]{2,1,0:T(2,128)(2,1)S(1)} async-done(((bf16[8,2,256]{2,1,0:T(2,128)(2,1)}), bf16[8,2,256]{2,1,0:T(2,128)(2,1)S(1)}, u32[]{:S(2)}, u32[]{:S(2)}) %all-to-all-start.2) | async-done | bytes 8224 | tf_op jit(solution)/shard_map/all_to_all | solution.py:33
  23.1 15.4 %all_to_all.51 = bf16[8,1,512,128]{3,2,1,0:T(8,128)(2,1)S(1)} all-to-all(bf16[8,1,512,128]{3,2,1,0:T(8,128)(2,1)S(1)} %get-tuple-element.6), channel_id=1, replica_groups=mesh['replica'=8,'fsdp'=32] {'replica'}, dimensions={0} | all-to-all | bytes 2097152 | tf_op jit(solution)/shard_map/all_to_all | solution.py:33
  38.5 0.0 copy-start
  38.5 0.0 copy-start.1
  38.5 3.7 %all-to-all-start.1 = ((bf16[8,1,512,128]{3,2,1,0:T(8,128)(2,1)}), bf16[8,1,512,128]{3,2,1,0:T(8,128)(2,1)S(1)}, u32[]{:S(2)}, u32[]{:S(2)}) async-start(bf16[8,1,512,128]{3,2,1,0:T(8,128)(2,1)} %get-tuple-element.7), calls=%async_computation.1 | async-start | bytes 2097152 | tf_op jit(solution)/shard_map/all_to_all | solution.py:33
  42.3 12.0 %all-to-all-done.1 = bf16[8,1,512,128]{3,2,1,0:T(8,128)(2,1)S(1)} async-done(((bf16[8,1,512,128]{3,2,1,0:T(8,128)(2,1)}), bf16[8,1,512,128]{3,2,1,0:T(8,128)(2,1)S(1)}, u32[]{:S(2)}, u32[]{:S(2)}) %all-to-all-start.1) | async-done | bytes 1048608 | tf_op jit(solution)/shard_map/all_to_all | solution.py:33
  54.4 1.8 %fusion = bf16[1024,128]{1,0:T(8,128)(2,1)S(1)} fusion(bf16[8,1,512,128]{3,2,1,0:T(8,128)(2,1)S(1)} %all-to-all-done.1, bf16[8,1,512,128]{3,2,1,0:T(8,128)(2,1)S(1)} %all_to_all.51, f32[8,1024]{1,0:T(8,128)S(1)} %bitcast.42), kind=kLoop, calls=%fused_computation.1 | loop fusion | flops 7208960 | bytes 2392064 | tf_op jit(solution)/shard_map/reduce_sum | solution.py:71
  56.1 28.0 %all_to_all.52 = bf16[32,32,128]{2,1,0:T(8,128)(2,1)S(1)} all-to-all(bf16[32,32,128]{2,1,0:T(8,128)(2,1)S(1)} %bitcast.39), channel_id=1, replica_groups=mesh['replica'=8,'fsdp'=32] {'fsdp'}, dimensions={0} | all-to-all | bytes 524288 | tf_op jit(solution)/shard_map/all_to_all | solution.py:72
  84.2 0.0 copy-done
  84.2 0.0 copy-done.1
  84.2 1.1 convert_bitcast_fusion
  85.4 16.8 %all_to_all.53 = bf16[32,32,128]{2,0,1:T(8,128)(2,1)S(1)} all-to-all(bf16[32,32,128]{2,0,1:T(8,128)(2,1)S(1)} %bitcast.41), channel_id=1, replica_groups=mesh['replica'=8,'fsdp'=32] {'fsdp'}, dimensions={1} | all-to-all | bytes 524288 | tf_op jit(solution)/shard_map/all_to_all | solution.py:77
  102.2 0.3 broadcast_in_dim.10
  102.5 28.7 %all_to_all.54 = bf16[8,1024,128]{2,1,0:T(8,128)(2,1)S(1)} all-to-all(bf16[8,1024,128]{2,1,0:T(8,128)(2,1)S(1)} %broadcast_in_dim.10), channel_id=1, replica_groups=mesh['replica'=8,'fsdp'=32] {'replica'}, dimensions={0} | all-to-all | bytes 4194304 | tf_op jit(solution)/shard_map/all_to_all | solution.py:39
  131.2 1.3 copy.23
  (6 shorter events, 0.2 us)
Async XLA Ops:
  3.3 11.0 %all-to-all-start.3 = ((bf16[8,2,256]{2,1,0:T(2,128)(2,1)}), bf16[8,2,256]{2,1,0:T(2,128)(2,1)S(1)}, u32[]{:S(2)}, u32[]{:S(2)}) async-start(bf16[8,2,256]{2,1,0:T(2,128)(2,1)} %reshape.73), calls=%async_computation.3 | async-start | bytes 16384 | tf_op jit(solution)/shard_map/all_to_all | solution.py:33
  14.3 8.9 %all-to-all-start.2 = ((bf16[8,2,256]{2,1,0:T(2,128)(2,1)}), bf16[8,2,256]{2,1,0:T(2,128)(2,1)S(1)}, u32[]{:S(2)}, u32[]{:S(2)}) async-start(bf16[8,2,256]{2,1,0:T(2,128)(2,1)} %reshape.75), calls=%async_computation.2 | async-start | bytes 16384 | tf_op jit(solution)/shard_map/all_to_all | solution.py:33
  38.5 45.7 %copy-start = (f32[32,4096]{1,0:T(8,128)S(1)}, f32[32,4096]{1,0:T(8,128)}, u32[]{:S(2)}) copy-start(f32[32,4096]{1,0:T(8,128)} %param.6) | copy-start | bytes 1572868
  38.5 45.7 %copy-start.1 = (f32[32,4096]{1,0:T(8,128)S(1)}, f32[32,4096]{1,0:T(8,128)}, u32[]{:S(2)}) copy-start(f32[32,4096]{1,0:T(8,128)} %param.7) | copy-start | bytes 1572868
  38.5 15.8 %all-to-all-start.1 = ((bf16[8,1,512,128]{3,2,1,0:T(8,128)(2,1)}), bf16[8,1,512,128]{3,2,1,0:T(8,128)(2,1)S(1)}, u32[]{:S(2)}, u32[]{:S(2)}) async-start(bf16[8,1,512,128]{3,2,1,0:T(8,128)(2,1)} %get-tuple-element.7), calls=%async_computation.1 | async-start | bytes 2097152 | tf_op jit(solution)/shard_map/all_to_all | solution.py:33
where the time goes:
time: 133 us
  blocking collectives  89 us (67%)
  waiting for transfers between devices  17.3 us (13%)
  starting transfers between devices  13.5 us (10%)
  other arithmetic  7.48 us (6%)
  local copies, waits for them, and re-layouts  4.59 us (3%)
    all_to_all x1, blocking collectives, copy_for_each(): lax.all_to_all(jnp.broadcast_to(x[None], (size, *x.shape)), axis, 0, 0, t...  28.7 us
    all_to_all x1, blocking collectives, local(): lax.all_to_all(partial_sum.astype(jnp.bfloat16), 'fsdp', split_axis=0, co...  28 us
    all_to_all x3, waiting for transfers between devices, several_exchanges(): lax.all_to_all(slab, axis, split_axis=0, concat_axis=0, tiled=True)  17.3 us
    all_to_all x1, blocking collectives, local(): lax.all_to_all(rounded, 'fsdp', split_axis=1, concat_axis=0, tiled=True)  16.8 us
    all_to_all x1, blocking collectives, several_exchanges(): lax.all_to_all(slab, axis, split_axis=0, concat_axis=0, tiled=True)  15.4 us
    all_to_all x3, starting transfers between devices, several_exchanges(): lax.all_to_all(slab, axis, split_axis=0, concat_axis=0, tiled=True)  13.5 us
    unnamed x11, local copies, waits for them, and re-layouts  3.09 us
  transfers between devices with their start and end apart: 3, of which 3 were waited for; matrix products, arithmetic and copies ran while one was open for 4% of the time, Pallas kernels for 0%

commit v1 on v0

v1 whole, which is shorter than its diff:
```python
import jax
import jax.numpy as jnp
from jax import lax
from jax.experimental import pallas as pl
from jax.experimental.pallas import tpu as pltpu
from jax.sharding import PartitionSpec as P


outer_rate = 0.7
momentum_factor = 0.9

ORDERS = ((0, 1, 2), (1, 2, 0), (2, 0, 1))
CUTS = (0, 352, 688, 1024)
SIZES = tuple(CUTS[k + 1] - CUTS[k] for k in range(3))
BLOCK = 1024
TILE = 128


def partner(r, direction):
    y, x = r // 2, r % 2
    if direction == 0:
        y = y ^ 1
    elif direction == 1:
        y = 3 - y
    else:
        x = x ^ 1
    return 2 * y + x


def swap(v, direction):
    return lax.ppermute(v, "replica", [(r, partner(r, direction)) for r in range(8)])


def away(steps):
    r = lax.axis_index("replica")
    y, x = lax.div(r, 2), lax.rem(r, 2)
    if steps[0]:
        y = jnp.bitwise_xor(y, 1)
    if steps[1]:
        y = 3 - y
    if steps[2]:
        x = 1 - x
    return 2 * y + x


def steps_of(k, first, j):
    steps = [0, 0, 0]
    for direction, bit in zip(ORDERS[k], (first, j // 2, j % 2)):
        steps[direction] = bit
    return steps


def dequant_kernel(first):
    def kernel(codes, scales, *refs):
        outs, buffers, sems = refs[:3], refs[3:6], refs[6]
        copies = []
        for k in range(3):
            for j in range(4):
                block = away(steps_of(k, first, j))
                start = pl.multiple_of(block * BLOCK + CUTS[k], 16)
                copy = pltpu.make_async_copy(
                    codes.at[pl.ds(start, SIZES[k])], buffers[k].at[j], sems.at[k, j]
                )
                copy.start()
                copies.append((k, j, block, copy))
        for k, j, block, copy in copies:
            copy.wait()
            low = CUTS[k]
            while low < CUTS[k + 1]:
                tile = low // TILE
                high = min((tile + 1) * TILE, CUTS[k + 1])
                row = scales[pl.ds(block * (BLOCK // TILE) + tile, 1), :]
                factor = jnp.transpose(jnp.broadcast_to(row, (TILE, TILE)))
                factor = factor[low - tile * TILE : high - tile * TILE]
                here = pl.ds(low - CUTS[k], high - low)
                values = buffers[k][j, here, :].astype(jnp.float32) * factor
                outs[k][j, here, :] = values.astype(outs[k].dtype)
                low = high

    return kernel


def dequant(codes, scales, first):
    return pl.pallas_call(
        dequant_kernel(first),
        out_shape=[pltpu.VMEM((4, n, 128), jnp.bfloat16) for n in SIZES],
        in_specs=[pl.BlockSpec(memory_space=pl.ANY), pl.BlockSpec(memory_space=pltpu.VMEM)],
        out_specs=[pl.BlockSpec(memory_space=pltpu.VMEM)] * 3,
        scratch_shapes=[pltpu.VMEM((4, n, 128), jnp.int32) for n in SIZES]
        + [pltpu.SemaphoreType.DMA((3, 4))],
        compiler_params=pltpu.CompilerParams(vmem_limit_bytes=8 << 20),
    )(codes, scales)


def place_kernel(first, aliased):
    def kernel(*refs):
        pieces, (out, sems) = refs[aliased : aliased + 3], refs[aliased + 3 :]
        copies = []
        for k in range(3):
            for j in range(4):
                start = pl.multiple_of(away(steps_of(k, first, j)) * BLOCK + CUTS[k], 16)
                copies.append(
                    pltpu.make_async_copy(
                        pieces[k].at[j], out.at[pl.ds(start, SIZES[k])], sems.at[k, j]
                    )
                )
        for copy in copies:
            copy.start()
        for copy in copies:
            copy.wait()

    return kernel


def place(pieces, first, out):
    aliased = 0 if out is None else 1
    return pl.pallas_call(
        place_kernel(first, aliased),
        out_shape=jax.ShapeDtypeStruct((8 * BLOCK, 128), jnp.bfloat16),
        in_specs=[pl.BlockSpec(memory_space=pl.ANY)] * aliased
        + [pl.BlockSpec(memory_space=pltpu.VMEM)] * 3,
        out_specs=pl.BlockSpec(memory_space=pl.ANY),
        scratch_shapes=[pltpu.SemaphoreType.DMA((3, 4))],
        input_output_aliases={0: 0} if aliased else {},
        compiler_params=pltpu.CompilerParams(vmem_limit_bytes=4 << 20),
    )(
        *([] if out is None else [out]),
        *[pltpu.with_memory_space_constraint(v, pltpu.VMEM) for v in pieces],
    )


def step(codes, scales, master, momentum):
    f32, bf16 = jnp.float32, jnp.bfloat16
    codes, scales = codes.reshape(8 * BLOCK, 128), scales.reshape(8 * BLOCK // TILE, TILE)
    sent = dequant(codes, scales, 1)
    got = []
    for k in range(3):
        got.append(swap(sent[k], ORDERS[k][0]))

    master_early, momentum_early = lax.optimization_barrier((master, momentum))
    q = master_early - (outer_rate * momentum_factor * momentum_factor) * momentum_early
    q = q.astype(bf16)
    q_columns = lax.all_to_all(q, "fsdp", split_axis=1, concat_axis=0, tiled=True)

    kept = dequant(codes, scales, 0)
    held = list(kept)
    for s in (1, 2):
        for k in range(3):
            v = held[k].astype(f32) + got[k].astype(f32)
            middle = v.shape[0] // 2
            got[k] = swap(v[middle:].astype(bf16), ORDERS[k][s])
            held[k] = v[:middle]
    total = [held[k][0] + got[k][0].astype(f32) for k in range(3)]

    weights = []
    for k in range(3):
        columns = q_columns[CUTS[k] : CUTS[k + 1]].astype(f32)
        w = columns - (outer_rate * (1 + momentum_factor) / 8) * total[k]
        weights.append(w.astype(bf16)[None])
    for s in (2, 1):
        for k in range(3):
            weights[k] = jnp.concatenate([weights[k], swap(weights[k], ORDERS[k][s])])
    others = []
    for k in range(3):
        others.append(swap(weights[k], ORDERS[k][0]))

    summed = jnp.concatenate(total).astype(bf16)
    summed = lax.all_to_all(summed, "fsdp", split_axis=0, concat_axis=1, tiled=True)
    mean = summed.astype(f32) / 8
    new_momentum = momentum_factor * momentum + mean
    new_master = master - outer_rate * (mean + momentum_factor * new_momentum)

    out = place(weights, 0, None)
    out = place(others, 1, out)
    return (new_master, new_momentum, out)


def solution(mesh):
    return jax.shard_map(
        step,
        mesh=mesh,
        in_specs=(
            P("replica", None, "fsdp"),
            P("replica", "fsdp", None),
            P(("replica", "fsdp"), None),
            P(("replica", "fsdp"), None),
        ),
        out_specs=(P(("replica", "fsdp"), None), P(("replica", "fsdp"), None), P(None, "fsdp")),
        check_vma=False,
    )
```

time: 133 us -> 86.2 us (0.65)
  blocking collectives: 89 us -> 0 us
  starting transfers between devices: 13.5 us -> 41.5 us
  Pallas kernels: 0 us -> 10.9 us
  local copies, waits for them, and re-layouts: 4.59 us -> 7.27 us
    all_to_all x4 -> x0, blocking collectives: 89 us -> none  [the longest x1 28.7 us: copy_for_each(): lax.all_to_all(jnp.broadcast_to(x[None], (size, *x.shape)), axis, 0, 0, t...]
    ppermute x0 -> x18, starting transfers between devices: none -> 16.9 us  [swap(): lax.ppermute(v, 'replica', [(r, partner(r, direction)) for r in range(8)])]
    all_to_all x3 -> x2, waiting for transfers between devices: 17.3 us -> 2.36 us  [the longest x1 1.46 us: step(): lax.all_to_all(q, 'fsdp', split_axis=1, concat_axis=0, tiled=True)]
    ppermute x0 -> x18, waiting for transfers between devices: none -> 14.7 us  [swap(): lax.ppermute(v, 'replica', [(r, partner(r, direction)) for r in range(8)])]
    all_to_all x3 -> x2, starting transfers between devices: 13.5 us -> 24.5 us  [the longest x1 12.5 us: step(): lax.all_to_all(summed, 'fsdp', split_axis=0, concat_axis=1, tiled=True)]
    pallas_call x0 -> x4, Pallas kernels: none -> 10.9 us  [the longest x2 8.82 us: dequant(): pl.pallas_call(dequant_kernel(first), out_shape=[pltpu.VMEM((4, n, 128),...]
    add x0 -> x6, other arithmetic: none -> 4.04 us  [step(): v = held[k].astype(f32) + got[k].astype(f32)]
    convert_element_type x3 -> x1, other arithmetic: 3.21 us -> 0.05 us  [step(): weights.append(w.astype(bf16)[None])]
  transfers between devices with their start and end apart: 3 -> 20, of which waited for: 3 -> 11; matrix products, arithmetic and copies ran while one was open for 4% -> 11% of each run, Pallas kernels for 0% -> 6%
where the time goes in v1:
time: 86.2 us; the launch traced here: 84.6 us
  starting transfers between devices  41.5 us (48%)
  waiting for transfers between devices  17.1 us (20%)
  Pallas kernels  10.9 us (13%)
  local copies, waits for them, and re-layouts  7.27 us (8%)
  other arithmetic  6.98 us (8%)
  between operations  0.89 us (1%)
    ppermute x18, starting transfers between devices, swap(): lax.ppermute(v, 'replica', [(r, partner(r, direction)) for r in range(8)])  16.9 us
    ppermute x18, waiting for transfers between devices, swap(): lax.ppermute(v, 'replica', [(r, partner(r, direction)) for r in range(8)])  14.7 us
    all_to_all x1, starting transfers between devices, step(): lax.all_to_all(summed, 'fsdp', split_axis=0, concat_axis=1, tiled=True)  12.5 us
    all_to_all x1, starting transfers between devices, step(): lax.all_to_all(q, 'fsdp', split_axis=1, concat_axis=0, tiled=True)  12 us
    pallas_call x2, Pallas kernels, dequant(): pl.pallas_call(dequant_kernel(first), out_shape=[pltpu.VMEM((4, n, 128),...  8.82 us
    unnamed x12, local copies, waits for them, and re-layouts  5.13 us
    add x6, other arithmetic, step(): v = held[k].astype(f32) + got[k].astype(f32)  4.04 us
    slice x6, local copies, waits for them, and re-layouts, step(): got[k] = swap(v[middle:].astype(bf16), ORDERS[k][s])  2.12 us
  transfers between devices with their start and end apart: 20, of which 11 were waited for; matrix products, arithmetic and copies ran while one was open for 11% of the time, Pallas kernels for 6%

profile of v1, /device:TPU:1, one launch (start us, length us, event | category | flops | bytes accessed | tf_op | source)
XLA Modules:
  0.0 84.6 jit_solution(16868165108602033810)
XLA Ops:
  0.6 0.0 copy-start
  0.6 2.2 %copy-done = s32[1,8192,128]{2,1,0:T(8,128)S(1)} copy-done((s32[1,8192,128]{2,1,0:T(8,128)S(1)}, s32[1,8192,128]{2,1,0:T(8,128)}, u32[]{:S(2)}) %copy-start) | copy-done | bytes 4194328
  2.8 0.8 copy-done.2
  3.6 4.4 %shard_map.68 = (bf16[4,352,128]{2,1,0:T(8,128)(2,1)S(1)}, bf16[4,336,128]{2,1,0:T(8,128)(2,1)S(1)}, bf16[4,336,128]{2,1,0:T(8,128)(2,1)S(1)}) custom-call(s32[8192,128]{1,0:T(8,128)S(1)} %bitcast.49, f32[64,128]{1,0:T(8,128)S(1)} %bitcast.51), custom_call_target="tpu_custom_call" | custom-call | tf_op jit(solution)/shard_map/pallas_call | solution.py:84
  8.0 3.6 %collective-permute-start.3 = (bf16[4,336,128]{2,1,0:T(8,128)(2,1)S(1)}, bf16[4,336,128]{2,1,0:T(8,128)(2,1)S(1)}, u32[]{:S(2)}, u32[]{:S(2)}) collective-permute-start(bf16[4,336,128]{2,1,0:T(8,128)(2,1)S(1)} %get-tuple-element.14), channel_id=1, source_target_pairs={{0,192},{32,224},{64,128},{96,160},{128,64},{160,96},{192,0},{224,... | collective-permute-start | bytes 1032200 | tf_op jit(solution)/shard_map/ppermute | solution.py:31
  11.7 1.2 %collective-permute-start.6 = (bf16[4,336,128]{2,1,0:T(8,128)(2,1)S(1)}, bf16[4,336,128]{2,1,0:T(8,128)(2,1)}, u32[]{:S(2)}, u32[]{:S(2)}) collective-permute-start(bf16[4,336,128]{2,1,0:T(8,128)(2,1)S(1)} %get-tuple-element.16), channel_id=1, source_target_pairs={{0,32},{32,0},{64,96},{96,64},{128,160},{160,128},{192,224},{224,1... | collective-permute-start | bytes 1032200 | tf_op jit(solution)/shard_map/ppermute | solution.py:31
  12.9 0.0 copy-done.4
  12.9 0.8 copy_bitcast_fusion
  13.6 12.0 %all-to-all-start.1 = ((bf16[32,32,128]{2,0,1:T(8,128)(2,1)}), bf16[32,32,128]{2,0,1:T(8,128)(2,1)S(1)}, u32[]{:S(2)}, u32[]{:S(2)}) async-start(bf16[32,32,128]{2,0,1:T(8,128)(2,1)} %copy_bitcast_fusion), calls=%async_computation.1 | async-start | bytes 524288 | tf_op jit(solution)/shard_map/all_to_all | solution.py:143
  25.7 0.1 collective-permute-start
  25.8 0.0 copy-start.1
  25.8 2.2 %copy-done.1 = s32[1,8192,128]{2,1,0:T(8,128)S(1)} copy-done((s32[1,8192,128]{2,1,0:T(8,128)S(1)}, s32[1,8192,128]{2,1,0:T(8,128)}, u32[]{:S(2)}) %copy-start.1) | copy-done | bytes 4194328
  28.0 4.4 %shard_map.67 = (bf16[4,352,128]{2,1,0:T(8,128)(2,1)S(1)}, bf16[4,336,128]{2,1,0:T(8,128)(2,1)S(1)}, bf16[4,336,128]{2,1,0:T(8,128)(2,1)S(1)}) custom-call(s32[8192,128]{1,0:T(8,128)S(1)} %bitcast.50, f32[64,128]{1,0:T(8,128)S(1)} %bitcast.52), custom_call_target="tpu_custom_call" | custom-call | tf_op jit(solution)/shard_map/pallas_call | solution.py:84
  32.4 0.0 collective-permute-done.3
  32.4 0.1 convert_add_fusion.2
  32.5 0.7 slice.120
  33.2 0.0 collective-permute-start.4
  33.2 0.0 collective-permute-done.6
  33.2 1.0 %convert_add_fusion.1 = f32[4,336,128]{2,1,0:T(8,128)S(1)} fusion(bf16[4,336,128]{2,1,0:T(8,128)(2,1)} %collective-permute-done.6, bf16[4,336,128]{2,1,0:T(8,128)(2,1)S(1)} %get-tuple-element.15), kind=kLoop, calls=%fused_computation.1 | loop fusion | flops 516096 | bytes 1376256 | tf_op jit(solution)/shard_map/add | solution.py:149
  34.2 0.7 slice.119
  34.9 1.4 %collective-permute-start.7 = (bf16[2,336,128]{2,1,0:T(8,128)(2,1)}, bf16[2,336,128]{2,1,0:T(8,128)(2,1)}, u32[]{:S(2)}, u32[]{:S(2)}) collective-permute-start(bf16[2,336,128]{2,1,0:T(8,128)(2,1)} %slice.119), channel_id=1, source_target_pairs={{0,64},{32,96},{64,0},{96,32},{128,192},{160,224},{192,128},{224,1... | collective-permute-start | bytes 516104 | tf_op jit(solution)/shard_map/ppermute | solution.py:31
  36.4 0.0 collective-permute-done
  36.4 0.1 convert_add_fusion
  36.4 0.7 slice.118
  37.1 0.0 collective-permute-start.1
  37.1 1.5 %all-to-all-done.1 = bf16[32,32,128]{2,0,1:T(8,128)(2,1)S(1)} async-done(((bf16[32,32,128]{2,0,1:T(8,128)(2,1)}), bf16[32,32,128]{2,0,1:T(8,128)(2,1)S(1)}, u32[]{:S(2)}, u32[]{:S(2)}) %all-to-all-start.1) | async-done | bytes 262176 | tf_op jit(solution)/shard_map/all_to_all | solution.py:143
  38.6 0.6 collective-permute-done.4
  39.2 0.9 %slice_add_fusion.2 = f32[2,336,128]{2,1,0:T(8,128)S(1)} fusion(f32[4,336,128]{2,1,0:T(8,128)S(1)} %convert_add_fusion.2, bf16[2,336,128]{2,1,0:T(8,128)(2,1)} %collective-permute-done.4), kind=kLoop, calls=%fused_computation.15 | loop fusion | flops 172032 | bytes 860160 | tf_op jit(solution)/shard_map/add | solution.py:149
  40.2 1.2 %collective-permute-start.5 = (bf16[1,336,128]{2,1,0:T(8,128)(2,1)S(1)}, bf16[1,336,128]{2,1,0:T(8,128)(2,1)S(1)}, u32[]{:S(2)}, u32[]{:S(2)}) collective-permute-start(bf16[1,336,128]{2,1,0:T(8,128)(2,1)S(1)} %slice.123), channel_id=1, source_target_pairs={{0,64},{32,96},{64,0},{96,32},{128,192},{160,224},{192,128},{224,1... | collective-permute-start | bytes 258056 | tf_op jit(solution)/shard_map/ppermute | solution.py:31
  41.4 0.0 collective-permute-done.7
  41.4 0.9 %slice_add_fusion.1 = f32[2,336,128]{2,1,0:T(8,128)S(1)} fusion(f32[4,336,128]{2,1,0:T(8,128)S(1)} %convert_add_fusion.1, bf16[2,336,128]{2,1,0:T(8,128)(2,1)} %collective-permute-done.7), kind=kLoop, calls=%fused_computation.13 | loop fusion | flops 172032 | bytes 860160 | tf_op jit(solution)/shard_map/add | solution.py:149
  42.4 0.1 collective-permute-start.8
  42.5 1.3 %collective-permute-done.1 = bf16[2,352,128]{2,1,0:T(8,128)(2,1)} collective-permute-done((bf16[2,352,128]{2,1,0:T(8,128)(2,1)}, bf16[2,352,128]{2,1,0:T(8,128)(2,1)}, u32[]{:S(2)}, u32[]{:S(2)}) %collective-permute-start.1) | collective-permute-done | bytes 180256 | tf_op jit(solution)/shard_map/ppermute | solution.py:31
  43.8 1.0 %slice_add_fusion = f32[2,352,128]{2,1,0:T(8,128)S(1)} fusion(f32[4,352,128]{2,1,0:T(8,128)S(1)} %convert_add_fusion, bf16[2,352,128]{2,1,0:T(8,128)(2,1)} %collective-permute-done.1), kind=kLoop, calls=%fused_computation.10 | loop fusion | flops 180224 | bytes 901120 | tf_op jit(solution)/shard_map/add | solution.py:149
  44.7 1.5 %collective-permute-start.2 = (bf16[1,352,128]{2,1,0:T(8,128)(2,1)S(1)}, bf16[1,352,128]{2,1,0:T(8,128)(2,1)S(1)}, u32[]{:S(2)}, u32[]{:S(2)}) collective-permute-start(bf16[1,352,128]{2,1,0:T(8,128)(2,1)S(1)} %slice.121), channel_id=1, source_target_pairs={{0,32},{32,0},{64,96},{96,64},{128,160},{160,128},{192,224},{224,1... | collective-permute-start | bytes 270344 | tf_op jit(solution)/shard_map/ppermute | solution.py:31
  46.2 0.0 collective-permute-done.5
  46.2 0.8 collective-permute-done.8
  47.0 0.1 fusion.13
  47.1 0.1 collective-permute-start.13
  47.2 0.1 collective-permute-start.11
  47.4 0.8 collective-permute-done.2
  48.2 0.1 fusion.3
  48.3 1.7 %collective-permute-start.9 = (bf16[1,352,128]{2,1,0:T(8,128)(2,1)S(1)}, bf16[1,352,128]{2,1,0:T(8,128)(2,1)S(1)}, u32[]{:S(2)}, u32[]{:S(2)}) collective-permute-start(bf16[1,352,128]{2,1,0:T(8,128)(2,1)S(1)} %get-tuple-element.21), channel_id=1, source_target_pairs={{0,32},{32,0},{64,96},{96,64},{128,160},{160,128},{192,224},{224,1... | collective-permute-start | bytes 270344 | tf_op jit(solution)/shard_map/ppermute | solution.py:31
  50.0 0.7 pad_maximum_fusion.3
  50.7 12.5 %all-to-all-start = ((bf16[32,32,128]{2,1,0:T(8,128)(2,1)}), bf16[32,32,128]{2,1,0:T(8,128)(2,1)S(1)}, u32[]{:S(2)}, u32[]{:S(2)}) async-start(bf16[32,32,128]{2,1,0:T(8,128)(2,1)} %bitcast.5), calls=%async_computation | async-start | bytes 524288 | tf_op jit(solution)/shard_map/all_to_all | solution.py:168
  63.2 0.0 collective-permute-done.13
  63.3 0.5 collective-permute-start.14
  63.8 0.0 collective-permute-done.11
  63.8 0.1 collective-permute-start.12
  63.9 0.0 collective-permute-done.9
  63.9 2.6 %collective-permute-start.10 = (bf16[2,352,128]{2,1,0:T(8,128)(2,1)S(1)}, bf16[2,352,128]{2,1,0:T(8,128)(2,1)S(1)}, u32[]{:S(2)}, u32[]{:S(2)}) collective-permute-start(bf16[2,352,128]{2,1,0:T(8,128)(2,1)S(1)} %pad_maximum_fusion.4), channel_id=1, source_target_pairs={{0,192},{32,224},{64,128},{96,160},{128,64},{160,96},{192,0},{224,... | collective-permute-start | bytes 540680 | tf_op jit(solution)/shard_map/ppermute | solution.py:31
  66.5 2.5 %collective-permute-done.14 = bf16[2,336,128]{2,1,0:T(8,128)(2,1)S(1)} collective-permute-done((bf16[2,336,128]{2,1,0:T(8,128)(2,1)S(1)}, bf16[2,336,128]{2,1,0:T(8,128)(2,1)S(1)}, u32[]{:S(2)}, u32[]{:S(2)}) %collective-permute-start.14) | collective-permute-done | bytes 172064 | tf_op jit(solution)/shard_map/ppermute | solution.py:31
  69.1 0.1 collective-permute-start.17
  69.2 2.3 %collective-permute-done.12 = bf16[2,336,128]{2,1,0:T(8,128)(2,1)S(1)} collective-permute-done((bf16[2,336,128]{2,1,0:T(8,128)(2,1)S(1)}, bf16[2,336,128]{2,1,0:T(8,128)(2,1)S(1)}, u32[]{:S(2)}, u32[]{:S(2)}) %collective-permute-start.12) | collective-permute-done | bytes 172064 | tf_op jit(solution)/shard_map/ppermute | solution.py:31
  71.5 2.5 %collective-permute-start.16 = (bf16[4,336,128]{2,1,0:T(8,128)(2,1)S(1)}, bf16[4,336,128]{2,1,0:T(8,128)(2,1)S(1)}, u32[]{:S(2)}, u32[]{:S(2)}) collective-permute-start(bf16[4,336,128]{2,1,0:T(8,128)(2,1)S(1)} %pad_maximum_fusion.1.refs_1_), channel_id=1, source_target_pairs={{0,192},{32,224},{64,128},{96,160},{128,64},{160,96},{192,0},{224,... | collective-permute-start | bytes 1032200 | tf_op jit(solution)/shard_map/ppermute | solution.py:31
  74.0 0.0 collective-permute-done.10
  74.1 1.1 %shard_map.69.refs_0_ = bf16[8192,128]{1,0:T(8,128)(2,1)} custom-call(bf16[4,352,128]{2,1,0:T(8,128)(2,1)S(1)} %pad_maximum_fusion.refs_0_, bf16[4,336,128]{2,1,0:T(8,128)(2,1)S(1)} %pad_maximum_fusion.1.refs_1_, bf16[4,336,128]{2,1,0:T(8,128)(2,1)S(1)} %pad_maximum_fusion.2.refs_2_), custom_call_target="tpu_custom_call" | custom-call | tf_op jit(solution)/shard_map/pallas_call | solution.py:117
  75.2 0.1 collective-permute-start.15
  75.3 0.9 %all-to-all-done = bf16[32,32,128]{2,1,0:T(8,128)(2,1)S(1)} async-done(((bf16[32,32,128]{2,1,0:T(8,128)(2,1)}), bf16[32,32,128]{2,1,0:T(8,128)(2,1)S(1)}, u32[]{:S(2)}, u32[]{:S(2)}) %all-to-all-start) | async-done | bytes 262176 | tf_op jit(solution)/shard_map/all_to_all | solution.py:168
  76.2 1.1 %fusion.1 = (f32[32,4096]{1,0:T(8,128)}, f32[32,4096]{1,0:T(8,128)}) fusion(f32[32,4096]{1,0:T(8,128)S(1)} %copy-done.4, f32[32,4096]{1,0:T(8,128)S(1)} %copy-done.5, bf16[32,32,128]{2,1,0:T(8,128)(2,1)S(1)} %all-to-all-done), kind=kLoop, calls=%fused_computation.6 | loop fusion | flops 1048576 | bytes 2359296 | tf_op jit(solution)/shard_map/sub | solution.py:171
  77.3 1.7 %collective-permute-done.17.refs_3_ = bf16[4,336,128]{2,1,0:T(8,128)(2,1)S(1)} collective-permute-done((bf16[4,336,128]{2,1,0:T(8,128)(2,1)S(1)}, bf16[4,336,128]{2,1,0:T(8,128)(2,1)S(1)}, u32[]{:S(2)}, u32[]{:S(2)}) %collective-permute-start.17) | collective-permute-done | bytes 344096 | tf_op jit(solution)/shard_map/ppermute | solution.py:31
  79.0 1.6 %collective-permute-done.16.refs_2_ = bf16[4,336,128]{2,1,0:T(8,128)(2,1)S(1)} collective-permute-done((bf16[4,336,128]{2,1,0:T(8,128)(2,1)S(1)}, bf16[4,336,128]{2,1,0:T(8,128)(2,1)S(1)}, u32[]{:S(2)}, u32[]{:S(2)}) %collective-permute-start.16) | collective-permute-done | bytes 344096 | tf_op jit(solution)/shard_map/ppermute | solution.py:31
  80.6 3.0 %collective-permute-done.15.refs_1_ = bf16[4,352,128]{2,1,0:T(8,128)(2,1)S(1)} collective-permute-done((bf16[4,352,128]{2,1,0:T(8,128)(2,1)S(1)}, bf16[4,352,128]{2,1,0:T(8,128)(2,1)S(1)}, u32[]{:S(2)}, u32[]{:S(2)}) %collective-permute-start.15) | collective-permute-done | bytes 360480 | tf_op jit(solution)/shard_map/ppermute | solution.py:31
  83.5 1.1 %shard_map.70 = bf16[8192,128]{1,0:T(8,128)(2,1)} custom-call(bf16[8192,128]{1,0:T(8,128)(2,1)} %shard_map.69.refs_0_, bf16[4,352,128]{2,1,0:T(8,128)(2,1)S(1)} %collective-permute-done.15.refs_1_, bf16[4,336,128]{2,1,0:T(8,128)(2,1)S(1)} %collective-permute-done.16.refs_2_, ...), custom_call_target="tpu_custom_call", output_to_operand_aliasing={{}: (0, {})} | custom-call | tf_op jit(solution)/shard_map/pallas_call | solution.py:117
  (18 shorter events, 0.3 us)
Async XLA Ops:
  0.6 2.2 %copy-start = (s32[1,8192,128]{2,1,0:T(8,128)S(1)}, s32[1,8192,128]{2,1,0:T(8,128)}, u32[]{:S(2)}) copy-start(s32[1,8192,128]{2,1,0:T(8,128)} %param.4) | copy-start | bytes 12582916
  2.8 0.8 copy-start.2
  3.6 9.3 %copy-start.4 = (f32[32,4096]{1,0:T(8,128)S(1)}, f32[32,4096]{1,0:T(8,128)}, u32[]{:S(2)}) copy-start(f32[32,4096]{1,0:T(8,128)} %param.6) | copy-start | bytes 1572868
  3.6 9.3 %copy-start.5 = (f32[32,4096]{1,0:T(8,128)S(1)}, f32[32,4096]{1,0:T(8,128)}, u32[]{:S(2)}) copy-start(f32[32,4096]{1,0:T(8,128)} %param.7) | copy-start | bytes 1572868
  3.6 22.2 %copy-start.3 = (f32[1,1,8192]{2,1,0:T(1,128)S(1)}, f32[1,1,8192]{2,1,0:T(1,128)}, u32[]{:S(2)}) copy-start(f32[1,1,8192]{2,1,0:T(1,128)} %param.5) | copy-start | bytes 98308
  8.0 24.4 %collective-permute-start.3 = (bf16[4,336,128]{2,1,0:T(8,128)(2,1)S(1)}, bf16[4,336,128]{2,1,0:T(8,128)(2,1)S(1)}, u32[]{:S(2)}, u32[]{:S(2)}) collective-permute-start(bf16[4,336,128]{2,1,0:T(8,128)(2,1)S(1)} %get-tuple-element.14), channel_id=1, source_target_pairs={{0,192},{32,224},{64,128},{96,160},{128,64},{160,96},{192,0},{224,... | collective-permute-start | bytes 1032200 | tf_op jit(solution)/shard_map/ppermute | solution.py:31
  11.7 21.5 %collective-permute-start.6 = (bf16[4,336,128]{2,1,0:T(8,128)(2,1)S(1)}, bf16[4,336,128]{2,1,0:T(8,128)(2,1)}, u32[]{:S(2)}, u32[]{:S(2)}) collective-permute-start(bf16[4,336,128]{2,1,0:T(8,128)(2,1)S(1)} %get-tuple-element.16), channel_id=1, source_target_pairs={{0,32},{32,0},{64,96},{96,64},{128,160},{160,128},{192,224},{224,1... | collective-permute-start | bytes 1032200 | tf_op jit(solution)/shard_map/ppermute | solution.py:31
  13.6 25.0 %all-to-all-start.1 = ((bf16[32,32,128]{2,0,1:T(8,128)(2,1)}), bf16[32,32,128]{2,0,1:T(8,128)(2,1)S(1)}, u32[]{:S(2)}, u32[]{:S(2)}) async-start(bf16[32,32,128]{2,0,1:T(8,128)(2,1)} %copy_bitcast_fusion), calls=%async_computation.1 | async-start | bytes 524288 | tf_op jit(solution)/shard_map/all_to_all | solution.py:143
  25.7 10.7 %collective-permute-start = (bf16[4,352,128]{2,1,0:T(8,128)(2,1)S(1)}, bf16[4,352,128]{2,1,0:T(8,128)(2,1)S(1)}, u32[]{:S(2)}, u32[]{:S(2)}) collective-permute-start(bf16[4,352,128]{2,1,0:T(8,128)(2,1)S(1)} %get-tuple-element.12), channel_id=1, source_target_pairs={{0,64},{32,96},{64,0},{96,32},{128,192},{160,224},{192,128},{224,1... | collective-permute-start | bytes 1081352 | tf_op jit(solution)/shard_map/ppermute | solution.py:31
  25.8 2.2 %copy-start.1 = (s32[1,8192,128]{2,1,0:T(8,128)S(1)}, s32[1,8192,128]{2,1,0:T(8,128)}, u32[]{:S(2)}) copy-start(s32[1,8192,128]{2,1,0:T(8,128)} %param.4) | copy-start | bytes 12582916
  33.2 6.1 %collective-permute-start.4 = (bf16[2,336,128]{2,1,0:T(8,128)(2,1)}, bf16[2,336,128]{2,1,0:T(8,128)(2,1)}, u32[]{:S(2)}, u32[]{:S(2)}) collective-permute-start(bf16[2,336,128]{2,1,0:T(8,128)(2,1)} %slice.120), channel_id=1, source_target_pairs={{0,32},{32,0},{64,96},{96,64},{128,160},{160,128},{192,224},{224,1... | collective-permute-start | bytes 516104 | tf_op jit(solution)/shard_map/ppermute | solution.py:31
  34.9 6.5 %collective-permute-start.7 = (bf16[2,336,128]{2,1,0:T(8,128)(2,1)}, bf16[2,336,128]{2,1,0:T(8,128)(2,1)}, u32[]{:S(2)}, u32[]{:S(2)}) collective-permute-start(bf16[2,336,128]{2,1,0:T(8,128)(2,1)} %slice.119), channel_id=1, source_target_pairs={{0,64},{32,96},{64,0},{96,32},{128,192},{160,224},{192,128},{224,1... | collective-permute-start | bytes 516104 | tf_op jit(solution)/shard_map/ppermute | solution.py:31
  37.1 6.6 %collective-permute-start.1 = (bf16[2,352,128]{2,1,0:T(8,128)(2,1)}, bf16[2,352,128]{2,1,0:T(8,128)(2,1)}, u32[]{:S(2)}, u32[]{:S(2)}) collective-permute-start(bf16[2,352,128]{2,1,0:T(8,128)(2,1)} %slice.118), channel_id=1, source_target_pairs={{0,192},{32,224},{64,128},{96,160},{128,64},{160,96},{192,0},{224,... | collective-permute-start | bytes 540680 | tf_op jit(solution)/shard_map/ppermute | solution.py:31
  40.2 6.0 %collective-permute-start.5 = (bf16[1,336,128]{2,1,0:T(8,128)(2,1)S(1)}, bf16[1,336,128]{2,1,0:T(8,128)(2,1)S(1)}, u32[]{:S(2)}, u32[]{:S(2)}) collective-permute-start(bf16[1,336,128]{2,1,0:T(8,128)(2,1)S(1)} %slice.123), channel_id=1, source_target_pairs={{0,64},{32,96},{64,0},{96,32},{128,192},{160,224},{192,128},{224,1... | collective-permute-start | bytes 258056 | tf_op jit(solution)/shard_map/ppermute | solution.py:31
  42.4 4.6 %collective-permute-start.8 = (bf16[1,336,128]{2,1,0:T(8,128)(2,1)S(1)}, bf16[1,336,128]{2,1,0:T(8,128)(2,1)S(1)}, u32[]{:S(2)}, u32[]{:S(2)}) collective-permute-start(bf16[1,336,128]{2,1,0:T(8,128)(2,1)S(1)} %slice.122), channel_id=1, source_target_pairs={{0,192},{32,224},{64,128},{96,160},{128,64},{160,96},{192,0},{224,... | collective-permute-start | bytes 258056 | tf_op jit(solution)/shard_map/ppermute | solution.py:31
  44.7 3.5 %collective-permute-start.2 = (bf16[1,352,128]{2,1,0:T(8,128)(2,1)S(1)}, bf16[1,352,128]{2,1,0:T(8,128)(2,1)S(1)}, u32[]{:S(2)}, u32[]{:S(2)}) collective-permute-start(bf16[1,352,128]{2,1,0:T(8,128)(2,1)S(1)} %slice.121), channel_id=1, source_target_pairs={{0,32},{32,0},{64,96},{96,64},{128,160},{160,128},{192,224},{224,1... | collective-permute-start | bytes 270344 | tf_op jit(solution)/shard_map/ppermute | solution.py:31
  47.1 16.1 %collective-permute-start.13 = (bf16[1,336,128]{2,1,0:T(8,128)(2,1)S(1)}, bf16[1,336,128]{2,1,0:T(8,128)(2,1)S(1)}, u32[]{:S(2)}, u32[]{:S(2)}) collective-permute-start(bf16[1,336,128]{2,1,0:T(8,128)(2,1)S(1)} %get-tuple-element.23), channel_id=1, source_target_pairs={{0,192},{32,224},{64,128},{96,160},{128,64},{160,96},{192,0},{224,... | collective-permute-start | bytes 258056 | tf_op jit(solution)/shard_map/ppermute | solution.py:31
  47.2 16.6 %collective-permute-start.11 = (bf16[1,336,128]{2,1,0:T(8,128)(2,1)S(1)}, bf16[1,336,128]{2,1,0:T(8,128)(2,1)S(1)}, u32[]{:S(2)}, u32[]{:S(2)}) collective-permute-start(bf16[1,336,128]{2,1,0:T(8,128)(2,1)S(1)} %get-tuple-element.24), channel_id=1, source_target_pairs={{0,64},{32,96},{64,0},{96,32},{128,192},{160,224},{192,128},{224,1... | collective-permute-start | bytes 258056 | tf_op jit(solution)/shard_map/ppermute | solution.py:31
  48.3 15.7 %collective-permute-start.9 = (bf16[1,352,128]{2,1,0:T(8,128)(2,1)S(1)}, bf16[1,352,128]{2,1,0:T(8,128)(2,1)S(1)}, u32[]{:S(2)}, u32[]{:S(2)}) collective-permute-start(bf16[1,352,128]{2,1,0:T(8,128)(2,1)S(1)} %get-tuple-element.21), channel_id=1, source_target_pairs={{0,32},{32,0},{64,96},{96,64},{128,160},{160,128},{192,224},{224,1... | collective-permute-start | bytes 270344 | tf_op jit(solution)/shard_map/ppermute | solution.py:31
  50.7 25.4 %all-to-all-start = ((bf16[32,32,128]{2,1,0:T(8,128)(2,1)}), bf16[32,32,128]{2,1,0:T(8,128)(2,1)S(1)}, u32[]{:S(2)}, u32[]{:S(2)}) async-start(bf16[32,32,128]{2,1,0:T(8,128)(2,1)} %bitcast.5), calls=%async_computation | async-start | bytes 524288 | tf_op jit(solution)/shard_map/all_to_all | solution.py:168
  63.3 5.8 %collective-permute-start.14 = (bf16[2,336,128]{2,1,0:T(8,128)(2,1)S(1)}, bf16[2,336,128]{2,1,0:T(8,128)(2,1)S(1)}, u32[]{:S(2)}, u32[]{:S(2)}) collective-permute-start(bf16[2,336,128]{2,1,0:T(8,128)(2,1)S(1)} %pad_maximum_fusion.6), channel_id=1, source_target_pairs={{0,64},{32,96},{64,0},{96,32},{128,192},{160,224},{192,128},{224,1... | collective-permute-start | bytes 516104 | tf_op jit(solution)/shard_map/ppermute | solution.py:31
  63.8 7.7 %collective-permute-start.12 = (bf16[2,336,128]{2,1,0:T(8,128)(2,1)S(1)}, bf16[2,336,128]{2,1,0:T(8,128)(2,1)S(1)}, u32[]{:S(2)}, u32[]{:S(2)}) collective-permute-start(bf16[2,336,128]{2,1,0:T(8,128)(2,1)S(1)} %pad_maximum_fusion.5), channel_id=1, source_target_pairs={{0,32},{32,0},{64,96},{96,64},{128,160},{160,128},{192,224},{224,1... | collective-permute-start | bytes 516104 | tf_op jit(solution)/shard_map/ppermute | solution.py:31
  63.9 10.1 %collective-permute-start.10 = (bf16[2,352,128]{2,1,0:T(8,128)(2,1)S(1)}, bf16[2,352,128]{2,1,0:T(8,128)(2,1)S(1)}, u32[]{:S(2)}, u32[]{:S(2)}) collective-permute-start(bf16[2,352,128]{2,1,0:T(8,128)(2,1)S(1)} %pad_maximum_fusion.4), channel_id=1, source_target_pairs={{0,192},{32,224},{64,128},{96,160},{128,64},{160,96},{192,0},{224,... | collective-permute-start | bytes 540680 | tf_op jit(solution)/shard_map/ppermute | solution.py:31
  69.1 9.9 %collective-permute-start.17 = (bf16[4,336,128]{2,1,0:T(8,128)(2,1)S(1)}, bf16[4,336,128]{2,1,0:T(8,128)(2,1)S(1)}, u32[]{:S(2)}, u32[]{:S(2)}) collective-permute-start(bf16[4,336,128]{2,1,0:T(8,128)(2,1)S(1)} %pad_maximum_fusion.2.refs_2_), channel_id=1, source_target_pairs={{0,32},{32,0},{64,96},{96,64},{128,160},{160,128},{192,224},{224,1... | collective-permute-start | bytes 1032200 | tf_op jit(solution)/shard_map/ppermute | solution.py:31
  71.5 9.0 %collective-permute-start.16 = (bf16[4,336,128]{2,1,0:T(8,128)(2,1)S(1)}, bf16[4,336,128]{2,1,0:T(8,128)(2,1)S(1)}, u32[]{:S(2)}, u32[]{:S(2)}) collective-permute-start(bf16[4,336,128]{2,1,0:T(8,128)(2,1)S(1)} %pad_maximum_fusion.1.refs_1_), channel_id=1, source_target_pairs={{0,192},{32,224},{64,128},{96,160},{128,64},{160,96},{192,0},{224,... | collective-permute-start | bytes 1032200 | tf_op jit(solution)/shard_map/ppermute | solution.py:31
  75.2 8.4 %collective-permute-start.15 = (bf16[4,352,128]{2,1,0:T(8,128)(2,1)S(1)}, bf16[4,352,128]{2,1,0:T(8,128)(2,1)S(1)}, u32[]{:S(2)}, u32[]{:S(2)}) collective-permute-start(bf16[4,352,128]{2,1,0:T(8,128)(2,1)S(1)} %pad_maximum_fusion.refs_0_), channel_id=1, source_target_pairs={{0,64},{32,96},{64,0},{96,32},{128,192},{160,224},{192,128},{224,1... | collective-permute-start | bytes 1081352 | tf_op jit(solution)/shard_map/ppermute | solution.py:31

commit v2 on v1

v2 whole, which is shorter than its diff:
```python
import jax
import jax.numpy as jnp
from jax import lax
from jax.experimental import pallas as pl
from jax.experimental.pallas import tpu as pltpu
from jax.sharding import Mesh, PartitionSpec as P


outer_rate = 0.7
momentum_factor = 0.9

ORDERS = ((0, 1, 2), (1, 2, 0), (2, 0, 1))
PARTS = len(ORDERS)
CUTS = (0, 352, 688, 1024)
SIZES = tuple(CUTS[k + 1] - CUTS[k] for k in range(PARTS))
BLOCK = 1024
TILE = 128


def partner(r, direction):
    y, x = r // 2, r % 2
    if direction == 0:
        y = y ^ 1
    elif direction == 1:
        y = 3 - y
    else:
        x = x ^ 1
    return 2 * y + x


def swap(v, direction):
    return lax.ppermute(v, "replica", [(r, partner(r, direction)) for r in range(8)])


def away(steps):
    r = lax.axis_index("replica")
    y, x = lax.div(r, 2), lax.rem(r, 2)
    if steps[0]:
        y = jnp.bitwise_xor(y, 1)
    if steps[1]:
        y = 3 - y
    if steps[2]:
        x = 1 - x
    return 2 * y + x


def steps_of(k, first, j):
    steps = [0, 0, 0]
    for direction, bit in zip(ORDERS[k], (first, j // 2, j % 2)):
        steps[direction] = bit
    return steps


SLOTS = tuple((s, z, c) for s in range(2) for z in range(8) for c in range(2))
WIDE = 128
TALL = 32


def mate(slot):
    s, z, c = slot
    return 4 * z + 2 * jnp.bitwise_xor(lax.axis_index("xh"), s) + c


def exchange(near, far):
    far = lax.ppermute(far, "xh", [(0, 1), (1, 0)])
    return lax.all_to_all(jnp.stack([near, far], axis=1), ("z", "c"), 0, 0, tiled=True)


def first_kernel(codes, scales, master, momentum, *refs):
    kept, sent, far_near = refs[:PARTS], refs[PARTS : 2 * PARTS], refs[2 * PARTS : 2 * PARTS + 2]
    buffer, factors, outer, sems, more = refs[2 * PARTS + 2 :]
    small = [
        pltpu.make_async_copy(master, outer.at[0], more.at[0]),
        pltpu.make_async_copy(momentum, outer.at[1], more.at[1]),
        pltpu.make_async_copy(scales, factors, more.at[2]),
    ]
    for copy in small:
        copy.start()
    copies = []
    for i in range(8):
        block = away((i // 4, i // 2 % 2, i % 2))
        start = pl.multiple_of(block * BLOCK, BLOCK)
        copy = pltpu.make_async_copy(codes.at[pl.ds(start, BLOCK)], buffer.at[i], sems.at[i])
        copy.start()
        copies.append((block, copy))
    for copy in small:
        copy.wait()
    for i, slot in enumerate(SLOTS):
        columns = pl.ds(pl.multiple_of(mate(slot) * WIDE, WIDE), WIDE)
        q = outer[0, :, columns] - (outer_rate * momentum_factor**2) * outer[1, :, columns]
        far_near[slot[0]][i % 16] = q.astype(jnp.bfloat16)
    for i, (block, copy) in enumerate(copies):
        copy.wait()
        steps = (i // 4, i // 2 % 2, i % 2)
        for tile in range(BLOCK // TILE):
            row = factors[pl.ds(block * (BLOCK // TILE) + tile, 1), :]
            factor = jnp.transpose(jnp.broadcast_to(row, (TILE, TILE)))
            base = tile * TILE
            for k, (first, second, third) in enumerate(ORDERS):
                low, high = max(base, CUTS[k]), min(base + TILE, CUTS[k + 1])
                if low < high:
                    out = (sent if steps[first] else kept)[k]
                    j = 2 * steps[second] + steps[third]
                    values = buffer[i, pl.ds(low, high - low), :].astype(jnp.float32)
                    values = values * factor[low - base : high - base]
                    out[j, pl.ds(low - CUTS[k], high - low), :] = values.astype(out.dtype)


def first(codes, scales, master, momentum):
    args = [pltpu.with_memory_space_constraint(v, pltpu.HBM) for v in (codes, scales, master, momentum)]
    out = pl.pallas_call(
        first_kernel,
        out_shape=[pltpu.VMEM((4, n, 128), jnp.bfloat16) for n in SIZES] * 2
        + [pltpu.VMEM((16, TALL, WIDE), jnp.bfloat16)] * 2,
        in_specs=[pl.BlockSpec(memory_space=pltpu.HBM)] * 4,
        out_specs=[pl.BlockSpec(memory_space=pltpu.VMEM)] * (2 * PARTS + 2),
        scratch_shapes=[
            pltpu.VMEM((8, BLOCK, 128), jnp.int32),
            pltpu.VMEM((8 * BLOCK // TILE, TILE), jnp.float32),
            pltpu.VMEM((2, *master.shape), jnp.float32),
            pltpu.SemaphoreType.DMA((8,)),
            pltpu.SemaphoreType.DMA((3,)),
        ],
        compiler_params=pltpu.CompilerParams(vmem_limit_bytes=12 << 20),
        name="first",
    )(*args)
    return list(out[:PARTS]), list(out[PARTS : 2 * PARTS]), out[2 * PARTS], out[2 * PARTS + 1]


def place_copies(pieces, first, out, sems):
    copies = []
    for k in range(PARTS):
        for j in range(4):
            start = pl.multiple_of(away(steps_of(k, first, j)) * BLOCK + CUTS[k], 16)
            rows = out.at[pl.ds(start, SIZES[k])]
            copies.append(pltpu.make_async_copy(pieces[k].at[j], rows, sems.at[k, j]))
    return copies


def place_kernel(*refs):
    copies = place_copies(refs[:PARTS], 0, *refs[PARTS:])
    for copy in copies:
        copy.start()
    for copy in copies:
        copy.wait()


def place(pieces):
    return pl.pallas_call(
        place_kernel,
        out_shape=jax.ShapeDtypeStruct((8 * BLOCK, 128), jnp.bfloat16),
        in_specs=[pl.BlockSpec(memory_space=pltpu.VMEM)] * PARTS,
        out_specs=pl.BlockSpec(memory_space=pl.ANY),
        scratch_shapes=[pltpu.SemaphoreType.DMA((PARTS, 4))],
        compiler_params=pltpu.CompilerParams(vmem_limit_bytes=4 << 20),
        name="place",
    )(*[pltpu.with_memory_space_constraint(v, pltpu.VMEM) for v in pieces])


def vmem_call(kernel, out_shape, args, limit=8):
    return pl.pallas_call(
        kernel,
        out_shape=out_shape,
        in_specs=[pl.BlockSpec(memory_space=pltpu.VMEM)] * len(args),
        out_specs=jax.tree.map(lambda _: pl.BlockSpec(memory_space=pltpu.VMEM), out_shape),
        compiler_params=pltpu.CompilerParams(vmem_limit_bytes=limit << 20),
    )(*args)


def rows_kernel(slots, out):
    for i, slot in enumerate(SLOTS):
        rows = pl.ds(pl.multiple_of(mate(slot) * TALL, TALL), TALL)
        out[rows, :] = slots[i % 16, slot[0]]


def slots_kernel(rows, near, far):
    for i, slot in enumerate(SLOTS):
        (far if slot[0] else near)[i % 16] = rows[pl.ds(pl.multiple_of(mate(slot) * TALL, TALL), TALL), :]


def add_kernel(kept, got, held, sent):
    half = kept.shape[0] // 2
    held[...] = kept[:half].astype(held.dtype) + got[:half].astype(held.dtype)
    v = kept[half:].astype(held.dtype) + got[half:].astype(held.dtype)
    sent[...] = v.astype(sent.dtype)


def last_kernel(slots, master, momentum, *refs):
    pieces, (_, out, new_master, new_momentum, sems) = refs[:PARTS], refs[PARTS:]
    copies = place_copies(pieces, 1, out, sems)
    for copy in copies:
        copy.start()
    for i, slot in enumerate(SLOTS):
        columns = pl.ds(pl.multiple_of(mate(slot) * WIDE, WIDE), WIDE)
        mean = slots[i % 16, slot[0]].astype(jnp.float32) / 8
        faster = momentum_factor * momentum[:, columns] + mean
        new_momentum[:, columns] = faster
        new_master[:, columns] = master[:, columns] - outer_rate * (mean + momentum_factor * faster)
    for copy in copies:
        copy.wait()


def last(slots, master, momentum, pieces, out):
    vmem = pl.BlockSpec(memory_space=pltpu.VMEM)
    hbm = pl.BlockSpec(memory_space=pl.ANY)
    pieces = [pltpu.with_memory_space_constraint(v, pltpu.VMEM) for v in pieces]
    return pl.pallas_call(
        last_kernel,
        out_shape=[jax.ShapeDtypeStruct(v.shape, v.dtype) for v in (out, master, momentum)],
        in_specs=[vmem] * (3 + PARTS) + [hbm],
        out_specs=[hbm, vmem, vmem],
        scratch_shapes=[pltpu.SemaphoreType.DMA((PARTS, 4))],
        input_output_aliases={3 + PARTS: 0},
        compiler_params=pltpu.CompilerParams(vmem_limit_bytes=10 << 20),
        name="last",
    )(slots, master, momentum, *pieces, out)


def step(codes, scales, master, momentum):
    f32, bf16 = jnp.float32, jnp.bfloat16
    codes, scales = codes.reshape(8 * BLOCK, 128), scales.reshape(8 * BLOCK // TILE, TILE)
    held, sent, near, far = first(codes, scales, master, momentum)
    got = []
    for k in range(PARTS):
        got.append(swap(sent[k], ORDERS[k][0]))

    q = exchange(near, far)
    for s in (1, 2):
        for k in range(PARTS):
            shape = (held[k].shape[0] // 2, *held[k].shape[1:])
            inputs = [pltpu.with_memory_space_constraint(v, pltpu.VMEM) for v in (held[k], got[k])]
            held[k], v = vmem_call(
                add_kernel, [pltpu.VMEM(shape, f32), pltpu.VMEM(shape, bf16)], inputs
            )
            got[k] = swap(v, ORDERS[k][s])
    total = [held[k][0] + got[k][0].astype(f32) for k in range(PARTS)]
    q = vmem_call(rows_kernel, pltpu.VMEM((BLOCK, WIDE), bf16), (q,))

    weights = []
    for k in range(PARTS):
        columns = q[CUTS[k] : CUTS[k + 1]].astype(f32)
        w = columns - (outer_rate * (1 + momentum_factor) / 8) * total[k]
        weights.append(w.astype(bf16)[None])
    for s in (2, 1):
        for k in range(PARTS):
            weights[k] = jnp.concatenate([weights[k], swap(weights[k], ORDERS[k][s])])
    others = []
    for k in range(PARTS):
        others.append(swap(weights[k], ORDERS[k][0]))

    near, far = vmem_call(
        slots_kernel,
        [pltpu.VMEM((16, TALL, WIDE), bf16)] * 2,
        (jnp.concatenate(total).astype(bf16),),
    )
    summed = exchange(near, far)
    out = place(weights)
    out, new_master, new_momentum = last(summed, master, momentum, others, out)
    return (new_master, new_momentum, out)


def solution(mesh):
    mesh = Mesh(mesh.devices.reshape(8, 8, 2, 2), ("replica", "z", "xh", "c"))
    fsdp = ("z", "xh", "c")
    return jax.shard_map(
        step,
        mesh=mesh,
        in_specs=(
            P("replica", None, fsdp),
            P("replica", fsdp, None),
            P(("replica", *fsdp), None),
            P(("replica", *fsdp), None),
        ),
        out_specs=(P(("replica", *fsdp), None), P(("replica", *fsdp), None), P(None, fsdp)),
        check_vma=False,
    )
```

time: 86.2 us -> 78.1 us (0.906); the launches traced: 84.6 us -> 77.7 us
  waiting for transfers between devices: 17.1 us -> 25.7 us
  local copies, waits for them, and re-layouts: 7.27 us -> 0.01 us
  other arithmetic: 6.98 us -> 1.83 us
  Pallas kernels: 10.9 us -> 7.75 us
    all_to_all x2, starting transfers between devices: 24.5 us -> 15.2 us  [exchange(): lax.all_to_all(jnp.stack([near, far], axis=1), ('z', 'c'), 0, 0, tiled=True)]
    ppermute x18, starting transfers between devices: 16.9 us -> 22.4 us  [swap(): lax.ppermute(v, 'replica', [(r, partner(r, direction)) for r in range(8)])]
    unnamed x12 -> x4, local copies, waits for them, and re-layouts: 5.13 us -> 0.01 us
    add x6 -> x0, other arithmetic: 4.04 us -> none  [step(): v = held[k].astype(f32) + got[k].astype(f32)]
    ppermute x0 -> x2, starting transfers between devices: none -> 3.96 us  [exchange(): far = lax.ppermute(far, 'xh', [(0, 1), (1, 0)])]
    all_to_all x2, waiting for transfers between devices: 2.36 us -> 6.25 us  [exchange(): lax.all_to_all(jnp.stack([near, far], axis=1), ('z', 'c'), 0, 0, tiled=True)]
    pallas_call x4 -> x11, Pallas kernels: 10.9 us -> 7.75 us  [the longest x1 4.08 us: first(): pl.pallas_call(first_kernel, out_shape=[pltpu.VMEM((4, n, 128), jnp.bfloa...]
    ppermute x18, waiting for transfers between devices: 14.7 us -> 17.1 us  [swap(): lax.ppermute(v, 'replica', [(r, partner(r, direction)) for r in range(8)])]
  transfers between devices with their start and end apart: 20 -> 22, of which waited for: 11 -> 10; matrix products, arithmetic and copies ran while one was open for 11% -> 2% of each run, Pallas kernels for 6% -> 2%
where the time goes in v2:
time: 78.1 us; the launch traced here: 77.7 us
  starting transfers between devices  41.5 us (53%)
  waiting for transfers between devices  25.7 us (33%)
  Pallas kernels  7.75 us (10%)
  other arithmetic  1.83 us (2%)
  between operations  0.84 us (1%)
    ppermute x18, starting transfers between devices, swap(): lax.ppermute(v, 'replica', [(r, partner(r, direction)) for r in range(8)])  22.4 us
    ppermute x18, waiting for transfers between devices, swap(): lax.ppermute(v, 'replica', [(r, partner(r, direction)) for r in range(8)])  17.1 us
    all_to_all x2, starting transfers between devices, exchange(): lax.all_to_all(jnp.stack([near, far], axis=1), ('z', 'c'), 0, 0, tiled=True)  15.2 us
    all_to_all x2, waiting for transfers between devices, exchange(): lax.all_to_all(jnp.stack([near, far], axis=1), ('z', 'c'), 0, 0, tiled=True)  6.25 us
    pallas_call x1, Pallas kernels, first(): pl.pallas_call(first_kernel, out_shape=[pltpu.VMEM((4, n, 128), jnp.bfloa...  4.08 us
    ppermute x2, starting transfers between devices, exchange(): far = lax.ppermute(far, 'xh', [(0, 1), (1, 0)])  3.96 us
    ppermute x2, waiting for transfers between devices, exchange(): far = lax.ppermute(far, 'xh', [(0, 1), (1, 0)])  2.35 us
    pallas_call x1, Pallas kernels, last(): pl.pallas_call(last_kernel, out_shape=[jax.ShapeDtypeStruct(v.shape, v.dt...  2.18 us
  transfers between devices with their start and end apart: 22, of which 10 were waited for; matrix products, arithmetic and copies ran while one was open for 2% of the time, Pallas kernels for 2%

profile of v2, /device:TPU:1, one launch (start us, length us, event | category | flops | bytes accessed | tf_op | source)
XLA Modules:
  0.0 77.7 jit_solution(6877077053973646913)
XLA Ops:
  0.6 4.1 %first.1 = (bf16[4,352,128]{2,1,0:T(8,128)(2,1)S(1)}, bf16[4,336,128]{2,1,0:T(8,128)(2,1)S(1)}, bf16[4,336,128]{2,1,0:T(8,128)(2,1)S(1)}, bf16[4,352,128]{2,1,0:...) custom-call(s32[8192,128]{1,0:T(8,128)} %bitcast.38, ...), custom_call_target="tpu_custom_call" | custom-call | tf_op jit(solution)/shard_map/first/pallas_call | solution.py:111
  4.7 3.7 %collective-permute-start.3 = (bf16[4,336,128]{2,1,0:T(8,128)(2,1)S(1)}, bf16[4,336,128]{2,1,0:T(8,128)(2,1)S(1)}, u32[]{:S(2)}, u32[]{:S(2)}) collective-permute-start(bf16[4,336,128]{2,1,0:T(8,128)(2,1)S(1)} %get-tuple-element.35), channel_id=1, source_target_pairs={{0,192},{32,224},{64,128},{96,160},{128,64},{160,96},{192,0},{224,... | collective-permute-start | bytes 1032200 | tf_op jit(solution)/shard_map/ppermute | solution.py:32
  8.4 0.0 collective-permute-start
  8.4 1.2 %collective-permute-start.6 = (bf16[4,336,128]{2,1,0:T(8,128)(2,1)S(1)}, bf16[4,336,128]{2,1,0:T(8,128)(2,1)S(1)}, u32[]{:S(2)}, u32[]{:S(2)}) collective-permute-start(bf16[4,336,128]{2,1,0:T(8,128)(2,1)S(1)} %get-tuple-element.41), channel_id=1, source_target_pairs={{0,32},{32,0},{64,96},{96,64},{128,160},{160,128},{192,224},{224,1... | collective-permute-start | bytes 1032200 | tf_op jit(solution)/shard_map/ppermute | solution.py:32
  9.6 5.5 %collective-permute-done.3.got = bf16[4,336,128]{2,1,0:T(8,128)(2,1)S(1)} collective-permute-done((bf16[4,336,128]{2,1,0:T(8,128)(2,1)S(1)}, bf16[4,336,128]{2,1,0:T(8,128)(2,1)S(1)}, u32[]{:S(2)}, u32[]{:S(2)}) %collective-permute-start.3) | collective-permute-done | bytes 344096 | tf_op jit(solution)/shard_map/ppermute | solution.py:32
  15.1 0.1 shard_map.69
  15.2 2.1 %collective-permute-start.4 = (bf16[2,336,128]{2,1,0:T(8,128)(2,1)S(1)}, bf16[2,336,128]{2,1,0:T(8,128)(2,1)S(1)}, u32[]{:S(2)}, u32[]{:S(2)}) collective-permute-start(bf16[2,336,128]{2,1,0:T(8,128)(2,1)S(1)} %get-tuple-element.37), channel_id=1, source_target_pairs={{0,32},{32,0},{64,96},{96,64},{128,160},{160,128},{192,224},{224,1... | collective-permute-start | bytes 516104 | tf_op jit(solution)/shard_map/ppermute | solution.py:32
  17.3 2.5 %collective-permute-start.10 = (bf16[16,32,128]{2,1,0:T(8,128)(2,1)S(1)}, bf16[16,32,128]{2,1,0:T(8,128)(2,1)S(1)}, u32[]{:S(2)}, u32[]{:S(2)}) collective-permute-start(bf16[16,32,128]{2,1,0:T(8,128)(2,1)S(1)} %get-tuple-element.49), channel_id=1, source_target_pairs={{0,2},{2,0},{1,3},{3,1},{4,6},{6,4},{5,7},{7,5},{8,10},{10,8},{9,1... | collective-permute-start | bytes 393224 | tf_op jit(solution)/shard_map/ppermute | solution.py:65
  19.8 0.0 collective-permute-done.got
  19.8 0.1 shard_map.67
  19.9 2.7 %collective-permute-start.1 = (bf16[2,352,128]{2,1,0:T(8,128)(2,1)S(1)}, bf16[2,352,128]{2,1,0:T(8,128)(2,1)S(1)}, u32[]{:S(2)}, u32[]{:S(2)}) collective-permute-start(bf16[2,352,128]{2,1,0:T(8,128)(2,1)S(1)} %get-tuple-element.31), channel_id=1, source_target_pairs={{0,192},{32,224},{64,128},{96,160},{128,64},{160,96},{192,0},{224,... | collective-permute-start | bytes 540680 | tf_op jit(solution)/shard_map/ppermute | solution.py:32
  22.5 0.0 collective-permute-done.6.got
  22.5 0.1 shard_map.71
  22.6 0.1 collective-permute-start.7
  22.7 0.0 collective-permute-done.4.got
  22.8 1.5 %collective-permute-start.5 = (bf16[1,336,128]{2,1,0:T(8,128)(2,1)S(1)}, bf16[1,336,128]{2,1,0:T(8,128)(2,1)S(1)}, u32[]{:S(2)}, u32[]{:S(2)}) collective-permute-start(bf16[1,336,128]{2,1,0:T(8,128)(2,1)S(1)} %get-tuple-element.39), channel_id=1, source_target_pairs={{0,64},{32,96},{64,0},{96,32},{128,192},{160,224},{192,128},{224,1... | collective-permute-start | bytes 258056 | tf_op jit(solution)/shard_map/ppermute | solution.py:32
  24.3 1.0 %collective-permute-done.10 = bf16[16,32,128]{2,1,0:T(8,128)(2,1)S(1)} collective-permute-done((bf16[16,32,128]{2,1,0:T(8,128)(2,1)S(1)}, bf16[16,32,128]{2,1,0:T(8,128)(2,1)S(1)}, u32[]{:S(2)}, u32[]{:S(2)}) %collective-permute-start.10) | collective-permute-done | bytes 131104 | tf_op jit(solution)/shard_map/ppermute | solution.py:65
  25.3 0.7 pad_maximum_fusion.5
  26.0 11.1 %all-to-all-start.1 = ((bf16[16,2,32,128]{3,2,1,0:T(8,128)(2,1)}), bf16[16,2,32,128]{3,2,1,0:T(8,128)(2,1)S(1)}, u32[]{:S(2)}, u32[]{:S(2)}) async-start(bf16[16,2,32,128]{3,2,1,0:T(8,128)(2,1)} %pad_maximum_fusion.5), calls=%async_computation.1 | async-start | bytes 524288 | tf_op jit(solution)/shard_map/all_to_all | solution.py:66
  37.1 0.0 collective-permute-done.7.got
  37.2 2.7 %collective-permute-start.8 = (bf16[1,336,128]{2,1,0:T(8,128)(2,1)S(1)}, bf16[1,336,128]{2,1,0:T(8,128)(2,1)S(1)}, u32[]{:S(2)}, u32[]{:S(2)}) collective-permute-start(bf16[1,336,128]{2,1,0:T(8,128)(2,1)S(1)} %get-tuple-element.45), channel_id=1, source_target_pairs={{0,192},{32,224},{64,128},{96,160},{128,64},{160,96},{192,0},{224,... | collective-permute-start | bytes 258056 | tf_op jit(solution)/shard_map/ppermute | solution.py:32
  39.8 0.0 collective-permute-done.1.got
  39.9 0.1 collective-permute-start.2
  40.0 0.0 collective-permute-done.5
  40.0 2.4 %collective-permute-done.8 = bf16[1,336,128]{2,1,0:T(8,128)(2,1)S(1)} collective-permute-done((bf16[1,336,128]{2,1,0:T(8,128)(2,1)S(1)}, bf16[1,336,128]{2,1,0:T(8,128)(2,1)S(1)}, u32[]{:S(2)}, u32[]{:S(2)}) %collective-permute-start.8) | collective-permute-done | bytes 86048 | tf_op jit(solution)/shard_map/ppermute | solution.py:32
  42.5 6.2 %all-to-all-done.1.slots = bf16[16,2,32,128]{3,2,1,0:T(8,128)(2,1)S(1)} async-done(((bf16[16,2,32,128]{3,2,1,0:T(8,128)(2,1)}), bf16[16,2,32,128]{3,2,1,0:T(8,128)(2,1)S(1)}, u32[]{:S(2)}, u32[]{:S(2)}) %all-to-all-start.1) | async-done | bytes 262176 | tf_op jit(solution)/shard_map/all_to_all | solution.py:66
  48.7 0.1 fusion.11
  48.8 2.7 %collective-permute-start.17 = (bf16[1,336,128]{2,1,0:T(8,128)(2,1)S(1)}, bf16[1,336,128]{2,1,0:T(8,128)(2,1)S(1)}, u32[]{:S(2)}, u32[]{:S(2)}) collective-permute-start(bf16[1,336,128]{2,1,0:T(8,128)(2,1)S(1)} %get-tuple-element.53), channel_id=1, source_target_pairs={{0,192},{32,224},{64,128},{96,160},{128,64},{160,96},{192,0},{224,... | collective-permute-start | bytes 258056 | tf_op jit(solution)/shard_map/ppermute | solution.py:32
  51.5 0.0 collective-permute-start.14
  51.5 0.0 collective-permute-done.2
  51.7 0.1 collective-permute-start.11
  51.8 1.5 %collective-permute-start.9 = (bf16[16,32,128]{2,1,0:T(8,128)(2,1)S(1)}, bf16[16,32,128]{2,1,0:T(8,128)(2,1)S(1)}, u32[]{:S(2)}, u32[]{:S(2)}) collective-permute-start(bf16[16,32,128]{2,1,0:T(8,128)(2,1)S(1)} %get-tuple-element.47), channel_id=1, source_target_pairs={{0,2},{2,0},{1,3},{3,1},{4,6},{6,4},{5,7},{7,5},{8,10},{10,8},{9,1... | collective-permute-start | bytes 393224 | tf_op jit(solution)/shard_map/ppermute | solution.py:65
  53.3 1.3 %collective-permute-done.17 = bf16[1,336,128]{2,1,0:T(8,128)(2,1)S(1)} collective-permute-done((bf16[1,336,128]{2,1,0:T(8,128)(2,1)S(1)}, bf16[1,336,128]{2,1,0:T(8,128)(2,1)S(1)}, u32[]{:S(2)}, u32[]{:S(2)}) %collective-permute-start.17) | collective-permute-done | bytes 86048 | tf_op jit(solution)/shard_map/ppermute | solution.py:32
  54.6 0.3 collective-permute-start.18
  54.9 0.8 %collective-permute-done.14 = bf16[1,336,128]{2,1,0:T(8,128)(2,1)S(1)} collective-permute-done((bf16[1,336,128]{2,1,0:T(8,128)(2,1)S(1)}, bf16[1,336,128]{2,1,0:T(8,128)(2,1)S(1)}, u32[]{:S(2)}, u32[]{:S(2)}) %collective-permute-start.14) | collective-permute-done | bytes 86048 | tf_op jit(solution)/shard_map/ppermute | solution.py:32
  55.7 0.1 collective-permute-start.15
  55.8 0.2 collective-permute-done.11
  56.0 1.5 %collective-permute-start.12 = (bf16[2,352,128]{2,1,0:T(8,128)(2,1)S(1)}, bf16[2,352,128]{2,1,0:T(8,128)(2,1)S(1)}, u32[]{:S(2)}, u32[]{:S(2)}) collective-permute-start(bf16[2,352,128]{2,1,0:T(8,128)(2,1)S(1)} %pad_maximum_fusion.6), channel_id=1, source_target_pairs={{0,192},{32,224},{64,128},{96,160},{128,64},{160,96},{192,0},{224,... | collective-permute-start | bytes 540680 | tf_op jit(solution)/shard_map/ppermute | solution.py:32
  57.5 1.3 %collective-permute-done.9 = bf16[16,32,128]{2,1,0:T(8,128)(2,1)S(1)} collective-permute-done((bf16[16,32,128]{2,1,0:T(8,128)(2,1)S(1)}, bf16[16,32,128]{2,1,0:T(8,128)(2,1)S(1)}, u32[]{:S(2)}, u32[]{:S(2)}) %collective-permute-start.9) | collective-permute-done | bytes 131104 | tf_op jit(solution)/shard_map/ppermute | solution.py:65
  58.9 0.7 pad_maximum_fusion.4
  59.6 4.1 %all-to-all-start = ((bf16[16,2,32,128]{3,2,1,0:T(8,128)(2,1)}), bf16[16,2,32,128]{3,2,1,0:T(8,128)(2,1)S(1)}, u32[]{:S(2)}, u32[]{:S(2)}) async-start(bf16[16,2,32,128]{3,2,1,0:T(8,128)(2,1)} %pad_maximum_fusion.4), calls=%async_computation | async-start | bytes 524288 | tf_op jit(solution)/shard_map/all_to_all | solution.py:66
  63.7 0.0 collective-permute-done.15
  63.8 0.7 collective-permute-start.16
  64.5 0.0 collective-permute-done.12
  64.5 0.0 copy-start
  64.5 0.0 copy-start.1
  64.5 1.6 %collective-permute-start.13 = (bf16[4,352,128]{2,1,0:T(8,128)(2,1)S(1)}, bf16[4,352,128]{2,1,0:T(8,128)(2,1)S(1)}, u32[]{:S(2)}, u32[]{:S(2)}) collective-permute-start(bf16[4,352,128]{2,1,0:T(8,128)(2,1)S(1)} %pad_maximum_fusion.refs_0_), channel_id=1, source_target_pairs={{0,64},{32,96},{64,0},{96,32},{128,192},{160,224},{192,128},{224,1... | collective-permute-start | bytes 1081352 | tf_op jit(solution)/shard_map/ppermute | solution.py:32
  66.1 0.0 collective-permute-done.18
  66.1 1.4 %collective-permute-start.19 = (bf16[4,336,128]{2,1,0:T(8,128)(2,1)S(1)}, bf16[4,336,128]{2,1,0:T(8,128)(2,1)S(1)}, u32[]{:S(2)}, u32[]{:S(2)}) collective-permute-start(bf16[4,336,128]{2,1,0:T(8,128)(2,1)S(1)} %pad_maximum_fusion.2.refs_2_), channel_id=1, source_target_pairs={{0,32},{32,0},{64,96},{96,64},{128,160},{160,128},{192,224},{224,1... | collective-permute-start | bytes 1032200 | tf_op jit(solution)/shard_map/ppermute | solution.py:32
  67.6 1.1 %place.1.refs_3_ = bf16[8192,128]{1,0:T(8,128)(2,1)} custom-call(bf16[4,352,128]{2,1,0:T(8,128)(2,1)S(1)} %pad_maximum_fusion.refs_0_, bf16[4,336,128]{2,1,0:T(8,128)(2,1)S(1)} %pad_maximum_fusion.1.refs_1_, bf16[4,336,128]{2,1,0:T(8,128)(2,1)S(1)} %pad_maximum_fusion.2.refs_2_), custom_call_target="tpu_custom_call" | custom-call | tf_op jit(solution)/shard_map/place/pallas_call | solution.py:149
  68.6 5.8 %collective-permute-done.16.refs_1_ = bf16[4,336,128]{2,1,0:T(8,128)(2,1)S(1)} collective-permute-done((bf16[4,336,128]{2,1,0:T(8,128)(2,1)S(1)}, bf16[4,336,128]{2,1,0:T(8,128)(2,1)S(1)}, u32[]{:S(2)}, u32[]{:S(2)}) %collective-permute-start.16) | collective-permute-done | bytes 344096 | tf_op jit(solution)/shard_map/ppermute | solution.py:32
  74.5 1.0 %collective-permute-done.19.refs_2_ = bf16[4,336,128]{2,1,0:T(8,128)(2,1)S(1)} collective-permute-done((bf16[4,336,128]{2,1,0:T(8,128)(2,1)S(1)}, bf16[4,336,128]{2,1,0:T(8,128)(2,1)S(1)}, u32[]{:S(2)}, u32[]{:S(2)}) %collective-permute-start.19) | collective-permute-done | bytes 344096 | tf_op jit(solution)/shard_map/ppermute | solution.py:32
  75.4 0.0 all-to-all-done.slots
  75.5 0.0 collective-permute-done.13.refs_0_
  75.5 0.0 copy-done
  75.5 0.0 copy-done.1
  75.5 2.2 %last.1 = (bf16[8192,128]{1,0:T(8,128)(2,1)}, f32[32,4096]{1,0:T(8,128)}, f32[32,4096]{1,0:T(8,128)}) custom-call(bf16[16,2,32,128]{3,2,1,0:T(8,128)(2,1)S(1)} %all-to-all-done.slots, f32[32,4096]{1,0:T(8,128)S(1)} %copy-done, f32[32,4096]{1,0:T(8,128)S(1)} %copy-done.1, ...), custom_call_target="tpu_custom_call", output_to_operand_aliasing={{0}: (6, {})} | custom-call | tf_op jit(solution)/shard_map/last/pallas_call | solution.py:207
  (16 shorter events, 0.5 us)
Async XLA Ops:
  4.7 10.4 %collective-permute-start.3 = (bf16[4,336,128]{2,1,0:T(8,128)(2,1)S(1)}, bf16[4,336,128]{2,1,0:T(8,128)(2,1)S(1)}, u32[]{:S(2)}, u32[]{:S(2)}) collective-permute-start(bf16[4,336,128]{2,1,0:T(8,128)(2,1)S(1)} %get-tuple-element.35), channel_id=1, source_target_pairs={{0,192},{32,224},{64,128},{96,160},{128,64},{160,96},{192,0},{224,... | collective-permute-start | bytes 1032200 | tf_op jit(solution)/shard_map/ppermute | solution.py:32
  8.4 11.4 %collective-permute-start = (bf16[4,352,128]{2,1,0:T(8,128)(2,1)S(1)}, bf16[4,352,128]{2,1,0:T(8,128)(2,1)S(1)}, u32[]{:S(2)}, u32[]{:S(2)}) collective-permute-start(bf16[4,352,128]{2,1,0:T(8,128)(2,1)S(1)} %get-tuple-element.29), channel_id=1, source_target_pairs={{0,64},{32,96},{64,0},{96,32},{128,192},{160,224},{192,128},{224,1... | collective-permute-start | bytes 1081352 | tf_op jit(solution)/shard_map/ppermute | solution.py:32
  8.4 14.2 %collective-permute-start.6 = (bf16[4,336,128]{2,1,0:T(8,128)(2,1)S(1)}, bf16[4,336,128]{2,1,0:T(8,128)(2,1)S(1)}, u32[]{:S(2)}, u32[]{:S(2)}) collective-permute-start(bf16[4,336,128]{2,1,0:T(8,128)(2,1)S(1)} %get-tuple-element.41), channel_id=1, source_target_pairs={{0,32},{32,0},{64,96},{96,64},{128,160},{160,128},{192,224},{224,1... | collective-permute-start | bytes 1032200 | tf_op jit(solution)/shard_map/ppermute | solution.py:32
  15.2 7.5 %collective-permute-start.4 = (bf16[2,336,128]{2,1,0:T(8,128)(2,1)S(1)}, bf16[2,336,128]{2,1,0:T(8,128)(2,1)S(1)}, u32[]{:S(2)}, u32[]{:S(2)}) collective-permute-start(bf16[2,336,128]{2,1,0:T(8,128)(2,1)S(1)} %get-tuple-element.37), channel_id=1, source_target_pairs={{0,32},{32,0},{64,96},{96,64},{128,160},{160,128},{192,224},{224,1... | collective-permute-start | bytes 516104 | tf_op jit(solution)/shard_map/ppermute | solution.py:32
  17.3 8.0 %collective-permute-start.10 = (bf16[16,32,128]{2,1,0:T(8,128)(2,1)S(1)}, bf16[16,32,128]{2,1,0:T(8,128)(2,1)S(1)}, u32[]{:S(2)}, u32[]{:S(2)}) collective-permute-start(bf16[16,32,128]{2,1,0:T(8,128)(2,1)S(1)} %get-tuple-element.49), channel_id=1, source_target_pairs={{0,2},{2,0},{1,3},{3,1},{4,6},{6,4},{5,7},{7,5},{8,10},{10,8},{9,1... | collective-permute-start | bytes 393224 | tf_op jit(solution)/shard_map/ppermute | solution.py:65
  19.9 20.0 %collective-permute-start.1 = (bf16[2,352,128]{2,1,0:T(8,128)(2,1)S(1)}, bf16[2,352,128]{2,1,0:T(8,128)(2,1)S(1)}, u32[]{:S(2)}, u32[]{:S(2)}) collective-permute-start(bf16[2,352,128]{2,1,0:T(8,128)(2,1)S(1)} %get-tuple-element.31), channel_id=1, source_target_pairs={{0,192},{32,224},{64,128},{96,160},{128,64},{160,96},{192,0},{224,... | collective-permute-start | bytes 540680 | tf_op jit(solution)/shard_map/ppermute | solution.py:32
  22.6 14.5 %collective-permute-start.7 = (bf16[2,336,128]{2,1,0:T(8,128)(2,1)S(1)}, bf16[2,336,128]{2,1,0:T(8,128)(2,1)S(1)}, u32[]{:S(2)}, u32[]{:S(2)}) collective-permute-start(bf16[2,336,128]{2,1,0:T(8,128)(2,1)S(1)} %get-tuple-element.43), channel_id=1, source_target_pairs={{0,64},{32,96},{64,0},{96,32},{128,192},{160,224},{192,128},{224,1... | collective-permute-start | bytes 516104 | tf_op jit(solution)/shard_map/ppermute | solution.py:32
  22.8 17.2 %collective-permute-start.5 = (bf16[1,336,128]{2,1,0:T(8,128)(2,1)S(1)}, bf16[1,336,128]{2,1,0:T(8,128)(2,1)S(1)}, u32[]{:S(2)}, u32[]{:S(2)}) collective-permute-start(bf16[1,336,128]{2,1,0:T(8,128)(2,1)S(1)} %get-tuple-element.39), channel_id=1, source_target_pairs={{0,64},{32,96},{64,0},{96,32},{128,192},{160,224},{192,128},{224,1... | collective-permute-start | bytes 258056 | tf_op jit(solution)/shard_map/ppermute | solution.py:32
  26.0 22.7 %all-to-all-start.1 = ((bf16[16,2,32,128]{3,2,1,0:T(8,128)(2,1)}), bf16[16,2,32,128]{3,2,1,0:T(8,128)(2,1)S(1)}, u32[]{:S(2)}, u32[]{:S(2)}) async-start(bf16[16,2,32,128]{3,2,1,0:T(8,128)(2,1)} %pad_maximum_fusion.5), calls=%async_computation.1 | async-start | bytes 524288 | tf_op jit(solution)/shard_map/all_to_all | solution.py:66
  37.2 5.3 %collective-permute-start.8 = (bf16[1,336,128]{2,1,0:T(8,128)(2,1)S(1)}, bf16[1,336,128]{2,1,0:T(8,128)(2,1)S(1)}, u32[]{:S(2)}, u32[]{:S(2)}) collective-permute-start(bf16[1,336,128]{2,1,0:T(8,128)(2,1)S(1)} %get-tuple-element.45), channel_id=1, source_target_pairs={{0,192},{32,224},{64,128},{96,160},{128,64},{160,96},{192,0},{224,... | collective-permute-start | bytes 258056 | tf_op jit(solution)/shard_map/ppermute | solution.py:32
  39.9 11.6 %collective-permute-start.2 = (bf16[1,352,128]{2,1,0:T(8,128)(2,1)S(1)}, bf16[1,352,128]{2,1,0:T(8,128)(2,1)S(1)}, u32[]{:S(2)}, u32[]{:S(2)}) collective-permute-start(bf16[1,352,128]{2,1,0:T(8,128)(2,1)S(1)} %get-tuple-element.33), channel_id=1, source_target_pairs={{0,32},{32,0},{64,96},{96,64},{128,160},{160,128},{192,224},{224,1... | collective-permute-start | bytes 270344 | tf_op jit(solution)/shard_map/ppermute | solution.py:32
  48.8 5.7 %collective-permute-start.17 = (bf16[1,336,128]{2,1,0:T(8,128)(2,1)S(1)}, bf16[1,336,128]{2,1,0:T(8,128)(2,1)S(1)}, u32[]{:S(2)}, u32[]{:S(2)}) collective-permute-start(bf16[1,336,128]{2,1,0:T(8,128)(2,1)S(1)} %get-tuple-element.53), channel_id=1, source_target_pairs={{0,192},{32,224},{64,128},{96,160},{128,64},{160,96},{192,0},{224,... | collective-permute-start | bytes 258056 | tf_op jit(solution)/shard_map/ppermute | solution.py:32
  51.5 4.2 %collective-permute-start.14 = (bf16[1,336,128]{2,1,0:T(8,128)(2,1)S(1)}, bf16[1,336,128]{2,1,0:T(8,128)(2,1)S(1)}, u32[]{:S(2)}, u32[]{:S(2)}) collective-permute-start(bf16[1,336,128]{2,1,0:T(8,128)(2,1)S(1)} %get-tuple-element.54), channel_id=1, source_target_pairs={{0,64},{32,96},{64,0},{96,32},{128,192},{160,224},{192,128},{224,1... | collective-permute-start | bytes 258056 | tf_op jit(solution)/shard_map/ppermute | solution.py:32
  51.7 4.3 %collective-permute-start.11 = (bf16[1,352,128]{2,1,0:T(8,128)(2,1)S(1)}, bf16[1,352,128]{2,1,0:T(8,128)(2,1)S(1)}, u32[]{:S(2)}, u32[]{:S(2)}) collective-permute-start(bf16[1,352,128]{2,1,0:T(8,128)(2,1)S(1)} %fusion.7), channel_id=1, source_target_pairs={{0,32},{32,0},{64,96},{96,64},{128,160},{160,128},{192,224},{224,1... | collective-permute-start | bytes 270344 | tf_op jit(solution)/shard_map/ppermute | solution.py:32
  51.8 7.1 %collective-permute-start.9 = (bf16[16,32,128]{2,1,0:T(8,128)(2,1)S(1)}, bf16[16,32,128]{2,1,0:T(8,128)(2,1)S(1)}, u32[]{:S(2)}, u32[]{:S(2)}) collective-permute-start(bf16[16,32,128]{2,1,0:T(8,128)(2,1)S(1)} %get-tuple-element.47), channel_id=1, source_target_pairs={{0,2},{2,0},{1,3},{3,1},{4,6},{6,4},{5,7},{7,5},{8,10},{10,8},{9,1... | collective-permute-start | bytes 393224 | tf_op jit(solution)/shard_map/ppermute | solution.py:65
  54.6 11.5 %collective-permute-start.18 = (bf16[2,336,128]{2,1,0:T(8,128)(2,1)S(1)}, bf16[2,336,128]{2,1,0:T(8,128)(2,1)S(1)}, u32[]{:S(2)}, u32[]{:S(2)}) collective-permute-start(bf16[2,336,128]{2,1,0:T(8,128)(2,1)S(1)} %pad_maximum_fusion.8), channel_id=1, source_target_pairs={{0,64},{32,96},{64,0},{96,32},{128,192},{160,224},{192,128},{224,1... | collective-permute-start | bytes 516104 | tf_op jit(solution)/shard_map/ppermute | solution.py:32
  55.7 8.0 %collective-permute-start.15 = (bf16[2,336,128]{2,1,0:T(8,128)(2,1)S(1)}, bf16[2,336,128]{2,1,0:T(8,128)(2,1)S(1)}, u32[]{:S(2)}, u32[]{:S(2)}) collective-permute-start(bf16[2,336,128]{2,1,0:T(8,128)(2,1)S(1)} %pad_maximum_fusion.7), channel_id=1, source_target_pairs={{0,32},{32,0},{64,96},{96,64},{128,160},{160,128},{192,224},{224,1... | collective-permute-start | bytes 516104 | tf_op jit(solution)/shard_map/ppermute | solution.py:32
  56.0 8.4 %collective-permute-start.12 = (bf16[2,352,128]{2,1,0:T(8,128)(2,1)S(1)}, bf16[2,352,128]{2,1,0:T(8,128)(2,1)S(1)}, u32[]{:S(2)}, u32[]{:S(2)}) collective-permute-start(bf16[2,352,128]{2,1,0:T(8,128)(2,1)S(1)} %pad_maximum_fusion.6), channel_id=1, source_target_pairs={{0,192},{32,224},{64,128},{96,160},{128,64},{160,96},{192,0},{224,... | collective-permute-start | bytes 540680 | tf_op jit(solution)/shard_map/ppermute | solution.py:32
  59.6 15.9 %all-to-all-start = ((bf16[16,2,32,128]{3,2,1,0:T(8,128)(2,1)}), bf16[16,2,32,128]{3,2,1,0:T(8,128)(2,1)S(1)}, u32[]{:S(2)}, u32[]{:S(2)}) async-start(bf16[16,2,32,128]{3,2,1,0:T(8,128)(2,1)} %pad_maximum_fusion.4), calls=%async_computation | async-start | bytes 524288 | tf_op jit(solution)/shard_map/all_to_all | solution.py:66
  63.8 10.7 %collective-permute-start.16 = (bf16[4,336,128]{2,1,0:T(8,128)(2,1)S(1)}, bf16[4,336,128]{2,1,0:T(8,128)(2,1)S(1)}, u32[]{:S(2)}, u32[]{:S(2)}) collective-permute-start(bf16[4,336,128]{2,1,0:T(8,128)(2,1)S(1)} %pad_maximum_fusion.1.refs_1_), channel_id=1, source_target_pairs={{0,192},{32,224},{64,128},{96,160},{128,64},{160,96},{192,0},{224,... | collective-permute-start | bytes 1032200 | tf_op jit(solution)/shard_map/ppermute | solution.py:32
  64.5 11.0 %copy-start = (f32[32,4096]{1,0:T(8,128)S(1)}, f32[32,4096]{1,0:T(8,128)}, u32[]{:S(2)}) copy-start(f32[32,4096]{1,0:T(8,128)} %master.3) | copy-start | bytes 1572868
  64.5 11.0 %copy-start.1 = (f32[32,4096]{1,0:T(8,128)S(1)}, f32[32,4096]{1,0:T(8,128)}, u32[]{:S(2)}) copy-start(f32[32,4096]{1,0:T(8,128)} %momentum.3) | copy-start | bytes 1572868
  64.5 10.9 %collective-permute-start.13 = (bf16[4,352,128]{2,1,0:T(8,128)(2,1)S(1)}, bf16[4,352,128]{2,1,0:T(8,128)(2,1)S(1)}, u32[]{:S(2)}, u32[]{:S(2)}) collective-permute-start(bf16[4,352,128]{2,1,0:T(8,128)(2,1)S(1)} %pad_maximum_fusion.refs_0_), channel_id=1, source_target_pairs={{0,64},{32,96},{64,0},{96,32},{128,192},{160,224},{192,128},{224,1... | collective-permute-start | bytes 1081352 | tf_op jit(solution)/shard_map/ppermute | solution.py:32
  66.1 9.3 %collective-permute-start.19 = (bf16[4,336,128]{2,1,0:T(8,128)(2,1)S(1)}, bf16[4,336,128]{2,1,0:T(8,128)(2,1)S(1)}, u32[]{:S(2)}, u32[]{:S(2)}) collective-permute-start(bf16[4,336,128]{2,1,0:T(8,128)(2,1)S(1)} %pad_maximum_fusion.2.refs_2_), channel_id=1, source_target_pairs={{0,32},{32,0},{64,96},{96,64},{128,160},{160,128},{192,224},{224,1... | collective-permute-start | bytes 1032200 | tf_op jit(solution)/shard_map/ppermute | solution.py:32
